TPU v7x, 128 devices: a whole 4x4x4 slice. The times are simulated.
128 devices in a mesh: col: 4 (over x), row: 32 (over z, y, core).
Axes of the slice: x: 4, y: 4, z: 4, core: 2. Of those that a mesh axis runs over, the one named last changes fastest.
Arguments:
- t_amps: float32 [1024, 20736], P('row', 'col')
- denoms: float32 [1024, 20736], P('row', 'col')
- v_oovv: bfloat16 [1024, 20736], P('row', 'col')
- v_vvvv: bfloat16 [20736, 20736], P('row', 'col')
- v_oooo: bfloat16 [1024, 1024], replicated
- w_direct: bfloat16 [4608, 4608], P(None, 'col')
- w_exch: bfloat16 [4608, 4608], P(None, 'col')
Outputs:
- output: float32 [1024, 20736], P('row', 'col')
All inputs are finite; a program needn't handle non-finite values.
Results may differ from a plain program's by a relative error of at most 0.001.
Values are sent between devices in bfloat16 or wider.
A program may use at most 1 GiB of HBM per device.

v0:
```python
import math
import jax
import jax.numpy as jnp
from jax import lax
from jax.sharding import PartitionSpec as P


def solution(mesh):
    n_row = mesh.shape["row"]
    n_col = mesh.shape["col"]
    amp_spec = P("row", "col")
    wide_spec = P(None, "col")

    def local_sweep(t_blk, d_blk, oovv_blk, vvvv_blk, oooo_full, wd_blk, wx_blk):
        rows_dev, cols_dev = t_blk.shape
        n_occ = math.isqrt(oooo_full.shape[0])
        n_virt = wd_blk.shape[0] // n_occ
        occ_row = n_occ // n_row
        occ_col = n_occ // n_col
        t_half = t_blk.astype(jnp.bfloat16)
        t_rows = lax.all_gather(t_half, "col", axis=1, tiled=True)
        t_ladder = lax.all_to_all(t_rows, "row", 1, 0, tiled=True)
        ladder_part = jnp.dot(t_ladder, vvvv_blk, preferred_element_type=jnp.float32)
        t_cols = lax.all_gather(t_half, "row", axis=0, tiled=True)
        x_part = lax.dot_general(oovv_blk, t_cols, (((1,), (1,)), ((), ())), preferred_element_type=jnp.float32)
        x_rows = lax.psum(x_part, "col")
        row_idx = lax.axis_index("row")
        oooo_rows = lax.dynamic_slice_in_dim(oooo_full, row_idx * rows_dev, rows_dev, axis=0)
        hole_mat = (oooo_rows.astype(jnp.float32) + 0.5 * x_rows).astype(jnp.bfloat16)
        hole_part = lax.dot_general(hole_mat, t_half, (((0,), (0,)), ((), ())), preferred_element_type=jnp.float32)
        ladder_sum = lax.psum_scatter(ladder_part + hole_part, "row", scatter_dimension=0, tiled=True)
        t_four = t_rows.reshape(occ_row, n_occ, n_virt, n_virt)
        direct_term = jnp.einsum("ikac,kcjb->ijab", t_four, wd_blk.reshape(n_occ, n_virt, occ_col, n_virt), preferred_element_type=jnp.float32)
        exch_term = jnp.einsum("ikcb,kcja->ijab", t_four, wx_blk.reshape(n_occ, n_virt, occ_col, n_virt), preferred_element_type=jnp.float32)
        ph_back = lax.all_to_all(direct_term - exch_term, "col", 2, 1, tiled=True)
        swap_row = lax.all_to_all(ph_back, "row", 1, 0, tiled=True)
        swap_both = lax.all_to_all(swap_row, "col", 3, 2, tiled=True)
        ph_sym = (ph_back + swap_both.transpose(1, 0, 3, 2)).reshape(rows_dev, cols_dev)
        residual = oovv_blk.astype(jnp.float32) + ladder_sum + ph_sym
        return residual / d_blk

    return jax.shard_map(local_sweep, mesh=mesh, in_specs=(amp_spec, amp_spec, amp_spec, amp_spec, P(), wide_spec, wide_spec), out_specs=amp_spec, check_vma=False)
```

profile of v0, /device:TPU:0, one launch (start us, length us, event | category | flops | bytes accessed | tf_op | source)
XLA Modules:
  0.0 371.7 jit_solution(10868414514002552122)
XLA Ops:
  6.5 1.9 convert_bitcast_fusion
  8.4 0.0 all-gather.6.cloned.1.call-update
  8.4 0.0 all-gather.4.cloned.1.call-start
  8.5 1.9 convert_element_type.13
  10.4 0.0 all-gather.4.cloned.1.call-update
  10.4 26.0 %all-gather.6.cloned.1.call-done = bf16[4,5184,32]{1,2,0:T(8,128)(2,1)} async-done(((bf16[1,5184,32]{1,2,0:T(8,128)(2,1)}), bf16[4,5184,32]{1,2,0:T(8,128)(2,1)}) %all-gather.6.cloned.1.call-update) | async-done | bytes 1327120 | tf_op jit(solution)/shard_map/all_gather | solution.py:21
  36.4 2.0 copy.42
  38.4 1.1 reshape.30
  39.5 3.7 %all_to_all.49 = bf16[32,32,648]{2,1,0:T(8,128)(2,1)S(1)} reshape(bf16[32,20736]{1,0:T(8,128)(2,1)S(1)} %bitcast.45) | data formatting | bytes 2654208 | tf_op jit(solution)/shard_map/all_to_all | solution.py:22
  43.3 2.0 copy.43
  45.3 7.4 %all-to-all-start = ((bf16[32,32,648]{2,0,1:T(8,128)(2,1)}), bf16[32,32,648]{2,0,1:T(8,128)(2,1)S(1)}, u32[]{:S(2)}, u32[]{:S(2)}) async-start(bf16[32,32,648]{2,0,1:T(8,128)(2,1)} %copy.43), calls=%async_computation | async-start | bytes 3145728 | tf_op jit(solution)/shard_map/all_to_all | solution.py:22
  52.7 0.0 all-reduce.2.cloned.1.call-start
  52.7 56.6 %all-gather.4.cloned.1.call-done = bf16[1024,5184]{1,0:T(8,128)(2,1)} async-done(((bf16[32,5184]{1,0:T(8,128)(2,1)}), bf16[1024,5184]{1,0:T(8,128)(2,1)}) %all-gather.4.cloned.1.call-update) | async-done | bytes 10616848 | tf_op jit(solution)/shard_map/all_gather | solution.py:24
  109.3 0.0 copy-done.2
  109.3 7.9 %fusion.18 = f32[32,1024]{1,0:T(8,128)} fusion(bf16[32,5184]{1,0:T(8,128)(2,1)S(1)} %copy-done.2, bf16[1024,5184]{1,0:T(8,128)(2,1)} %all-gather.4.cloned.1.call-done), kind=kOutput, calls=%fused_computation.17 | convolution fusion | flops 339738624 | bytes 11079680 | tf_op jit(solution)/shard_map/dot_general | solution.py:25
  117.2 0.0 all-reduce.2.cloned.1.call-update
  117.2 0.2 reduce-scatter.2.cloned.1.call-start
  117.4 0.0 all-to-all-done
  117.5 15.1 %fusion.17 = f32[1024,5184]{1,0:T(8,128)} fusion(bf16[1024,648]{1,0:T(8,128)(2,1)S(1)} %bitcast.54, bf16[648,5184]{1,0:T(8,128)(2,1)} %param.10), kind=kOutput, calls=%fused_computation.16 | convolution fusion | flops 6879707136 | bytes 29279232 | tf_op jit(solution)/shard_map/dot_general | solution.py:23
  132.6 25.6 %all-reduce.2.cloned.1.call-done = f32[32,1024]{1,0:T(8,128)} async-done(((f32[32,1024]{1,0:T(8,128)}), f32[32,1024]{1,0:T(8,128)}) %all-reduce.2.cloned.1.call-update) | async-done | bytes 131088 | tf_op jit(solution)/shard_map/psum | solution.py:26
  158.1 17.4 %convolution_add_fusion = f32[1024,5184]{1,0:T(8,128)} fusion(f32[1024,5184]{1,0:T(8,128)} %fusion.17, bf16[32,5184]{1,0:T(8,128)(2,1)S(1)} %copy-done, f32[32,1024]{1,0:T(8,128)} %all-reduce.2.cloned.1.call-done, bf16[1024,1024]{1,0:T(8,128)(2,1)} %param.11, s32[]{:T(128)S(6)} %select_n.3), kind=kOutput, calls=%fused_computation.4 | convolution fusion | flops 345178112 | bytes 43257860 | tf_op jit(solution)/shard_map/dot_general | solution.py:30
  175.5 0.0 reduce-scatter.2.cloned.1.call-update
  175.5 32.8 %reshape.27 = bf16[32,144,8,144]{3,2,1,0:T(8,128)(2,1)} reshape(bf16[4608,1152]{1,0:T(8,128)(2,1)} %param.13) | data formatting | bytes 21233664 | tf_op jit(solution)/shard_map/reshape | solution.py:34
  208.3 32.8 %reshape.25 = bf16[32,144,8,144]{3,2,1,0:T(8,128)(2,1)} reshape(bf16[4608,1152]{1,0:T(8,128)(2,1)} %param.12) | data formatting | bytes 21233664 | tf_op jit(solution)/shard_map/reshape | solution.py:33
  241.1 5.1 %reshape.31 = bf16[32,144,144,1]{2,1,0,3:T(8,128)(2,1)} reshape(bf16[32,20736]{1,0:T(8,128)(2,1)S(1)} %bitcast.46) | data formatting | bytes 2654208 | tf_op jit(solution)/shard_map/reshape
  246.2 13.5 %fusion.10 = f32[1,8,144,144]{2,3,1,0:T(8,128)S(1)} fusion(bf16[32,144,144,1]{2,1,0,3:T(8,128)(2,1)} %reshape.31, bf16[32,144,8,144]{3,2,1,0:T(8,128)(2,1)} %reshape.27), kind=kOutput, calls=%fused_computation.7 | convolution fusion | flops 1528823808 | bytes 12607488 | tf_op jit(solution)/shard_map/ikcb,kcja->ijab/dot_general | solution.py:34
  259.7 13.9 %fusion.7 = f32[1,8,144,144]{2,3,1,0:T(8,128)S(1)} fusion(f32[1,8,144,144]{2,3,1,0:T(8,128)S(1)} %fusion.10, bf16[32,144,144,1]{2,1,0,3:T(8,128)(2,1)S(1)} %copy-done.1, bf16[32,144,8,144]{3,2,1,0:T(8,128)(2,1)} %reshape.25), kind=kOutput, calls=%fused_computation.6 | convolution fusion | flops 1528989696 | bytes 13271040 | tf_op jit(solution)/shard_map/ikac,kcjb->ijab/dot_general | solution.py:33
  273.6 0.7 copy.47
  274.3 17.9 %all_to_all.67 = f32[1,8,144,144]{3,1,0,2:T(8,128)S(1)} all-to-all(f32[1,8,144,144]{3,1,0,2:T(8,128)S(1)} %copy.47), channel_id=1, replica_groups=mesh['col'=4,'row'=32] {'col'}, dimensions={2} | all-to-all | bytes 1327104 | tf_op jit(solution)/shard_map/all_to_all | solution.py:35
  292.3 0.1 copy.71
  292.4 1.2 copy.49
  293.6 26.7 %all_to_all.68 = f32[1,32,36,144]{3,0,2,1:T(1,128)} all-to-all(f32[1,32,36,144]{3,0,2,1:T(1,128)S(1)} %copy.49), channel_id=1, replica_groups=mesh['col'=4,'row'=32] {'row'}, dimensions={1} | all-to-all | bytes 1327104 | tf_op jit(solution)/shard_map/all_to_all | solution.py:36
  320.3 3.0 copy.50
  323.2 3.6 reshape.35
  326.9 15.4 %all_to_all.69 = f32[4,1,41472]{2,1,0:T(1,128)S(1)} all-to-all(f32[4,1,41472]{2,1,0:T(1,128)} %reshape.35), channel_id=1, replica_groups=mesh['col'=4,'row'=32] {'col'}, dimensions={0} | all-to-all | bytes 1327104 | tf_op jit(solution)/shard_map/all_to_all | solution.py:37
  342.2 0.5 broadcast
  342.7 3.3 reduce
  346.0 4.2 %reshape.36 = f32[144,1,32,36]{3,2,1,0:T(8,128)S(1)} reshape(f32[4,41472]{1,0:T(4,128)} %reduce) | data formatting | bytes 1327104
  350.2 3.7 copy.57
  353.9 4.5 %copy.52 = f32[32,1,4,36,36]{3,2,0,4,1:T(4,128)S(1)} copy(f32[32,1,4,36,36]{4,2,0,3,1:T(4,128)} %bitcast.51) | data formatting | bytes 1327104 | tf_op jit(solution)/shard_map/all_to_all | solution.py:37
  358.3 2.1 all_to_all.62
  360.4 1.4 bitcast_add_fusion
  361.8 0.0 copy-start.3
  361.9 0.0 copy-start.4
  361.9 0.7 copy.53
  362.6 0.5 reshape.28
  363.1 0.0 reduce-scatter.2.cloned.1.call-done
  363.1 2.1 add_divide_fusion
  (8 shorter events, 0.0 us)
Async XLA Ops:
  6.5 29.9 %all-gather.6.cloned.1.call-start = ((), (), s32[]{:S(2)}) async-start(), calls=%async_computation.8 | async-start | bytes 1679360 | tf_op jit(solution)/shard_map/all_gather | solution.py:21
  8.4 100.9 %all-gather.4.cloned.1.call-start = ((), (), s32[]{:S(2)}) async-start(), calls=%async_computation.5 | async-start | bytes 11083776 | tf_op jit(solution)/shard_map/all_gather | solution.py:24
  45.3 64.0 %copy-start.2 = (bf16[32,5184]{1,0:T(8,128)(2,1)S(1)}, bf16[32,5184]{1,0:T(8,128)(2,1)}, u32[]{:S(2)}) copy-start(bf16[32,5184]{1,0:T(8,128)(2,1)} %param.9) | copy-start | bytes 995332
  45.3 72.2 %all-to-all-start = ((bf16[32,32,648]{2,0,1:T(8,128)(2,1)}), bf16[32,32,648]{2,0,1:T(8,128)(2,1)S(1)}, u32[]{:S(2)}, u32[]{:S(2)}) async-start(bf16[32,32,648]{2,0,1:T(8,128)(2,1)} %copy.43), calls=%async_computation | async-start | bytes 3145728 | tf_op jit(solution)/shard_map/all_to_all | solution.py:22
  52.7 105.5 %all-reduce.2.cloned.1.call-start = ((), (), s32[]{:S(2)}) async-start(), calls=%async_computation.6 | async-start | bytes 262144 | tf_op jit(solution)/shard_map/psum | solution.py:26
  117.2 245.9 %reduce-scatter.2.cloned.1.call-start = ((), (), s32[]{:S(2)}) async-start(), calls=%async_computation.7 | async-start | bytes 22167552 | tf_op jit(solution)/shard_map/reduce_scatter | solution.py:31
  117.5 40.7 %copy-start = (bf16[32,5184]{1,0:T(8,128)(2,1)S(1)}, bf16[32,5184]{1,0:T(8,128)(2,1)}, u32[]{:S(2)}) copy-start(bf16[32,5184]{1,0:T(8,128)(2,1)} %convert_element_type.13) | copy-start | bytes 995332
  246.2 13.5 %copy-start.1 = (bf16[32,144,144,1]{2,1,0,3:T(8,128)(2,1)S(1)}, bf16[32,144,144,1]{2,1,0,3:T(8,128)(2,1)}, u32[]{:S(2)}) copy-start(bf16[32,144,144,1]{2,1,0,3:T(8,128)(2,1)} %reshape.31) | copy-start | bytes 3981316
  361.8 1.2 copy-start.3
  361.9 1.2 copy-start.4
Sparse Core Ops, SparseCore 0:
  9.0 27.3 all-gather.5
  38.6 70.6 all-gather.3
  117.3 40.7 all-reduce.1
  175.7 133.0 reduce-scatter.1
where the time goes:
time: 374 us; the launch traced here: 372 us
  waiting for transfers between devices  108 us (29%)
  local copies, waits for them, and re-layouts  104 us (28%)
  matrix products  67.7 us (18%)
  blocking collectives  60 us (16%)
  between operations  13.3 us (4%)
  other arithmetic  10.6 us (3%)
  starting transfers between devices  7.7 us (2%)
    all_gather x1, waiting for transfers between devices, local_sweep(): t_cols = lax.all_gather(t_half, 'row', axis=0, tiled=True)  56.6 us
    reshape x1, local copies, waits for them, and re-layouts, local_sweep(): wd_blk.reshape(n_occ, n_virt, occ_col, n_virt)  32.8 us
    reshape x1, local copies, waits for them, and re-layouts, local_sweep(): wx_blk.reshape(n_occ, n_virt, occ_col, n_virt)  32.8 us
    all_to_all x1, blocking collectives, local_sweep(): swap_row = lax.all_to_all(ph_back, 'row', 1, 0, tiled=True)  26.7 us
    all_gather x1, waiting for transfers between devices, local_sweep(): t_rows = lax.all_gather(t_half, 'col', axis=1, tiled=True)  26 us
    psum x1, waiting for transfers between devices, local_sweep(): x_rows = lax.psum(x_part, 'col')  25.6 us
    all_to_all x1, blocking collectives, local_sweep(): ph_back = lax.all_to_all(direct_term - exch_term, 'col', 2, 1, tiled=True)  17.9 us
    dot_general x1, matrix products, local_sweep(): lax.dot_general(hole_mat, t_half, (((0,), (0,)), ((), ())), preferred_ele...  17.4 us
  transfers between devices with their start and end apart: 5, of which 3 were waited for; matrix products, arithmetic and copies ran while one was open for 42% of the time, Pallas kernels for 0%

commit v1 on v0

v1 whole, which is shorter than its diff:
```python
import math
import jax
import jax.numpy as jnp
from jax import lax
from jax.sharding import PartitionSpec as P


def solution(mesh):
    n_row = mesh.shape["row"]
    n_col = mesh.shape["col"]
    amp_spec = P("row", "col")
    wide_spec = P(None, "col")

    def local_sweep(t_blk, d_blk, oovv_blk, vvvv_blk, oooo_full, wd_blk, wx_blk):
        f32 = jnp.float32
        rows_dev, cols_dev = t_blk.shape
        n_occ = math.isqrt(oooo_full.shape[0])
        n_virt = wd_blk.shape[0] // n_occ
        occ_col = n_occ // n_col
        virt_col = n_virt // n_col
        c_dev = vvvv_blk.shape[0]
        row_idx = lax.axis_index("row")
        t_half = t_blk.astype(jnp.bfloat16)
        t_rows = lax.all_gather(t_half, "col", axis=1, tiled=True)
        v_rows = lax.all_to_all(oovv_blk, "col", 0, 1, tiled=True)
        both = jnp.concatenate([t_rows, v_rows], axis=0)
        both = lax.all_to_all(both.reshape(rows_dev + occ_col, n_row, c_dev), "row", 1, 0, tiled=True)
        both = both.reshape(n_row, rows_dev + occ_col, c_dev)
        t_ladder = both[:, :rows_dev].reshape(n_row * rows_dev, c_dev)
        v_lad = both[:, rows_dev:].reshape(n_row * occ_col, c_dev)
        x_part = lax.dot_general(v_lad, t_ladder, (((1,), (1,)), ((), ())), preferred_element_type=f32)
        x_own = lax.psum_scatter(x_part, "row", scatter_dimension=0, tiled=True)
        start = row_idx * rows_dev + lax.axis_index("col") * occ_col
        oooo_rows = lax.dynamic_slice_in_dim(oooo_full, start, occ_col, axis=0)
        m_own = (oooo_rows.astype(f32) + 0.5 * x_own).astype(jnp.bfloat16)
        hole_mat = lax.all_gather(m_own, "col", axis=0, tiled=True)
        ladder_part = jnp.dot(t_ladder, vvvv_blk, preferred_element_type=f32)
        hole_part = lax.dot_general(hole_mat, t_half, (((0,), (0,)), ((), ())), preferred_element_type=f32)
        ladder_sum = lax.psum_scatter(ladder_part + hole_part, "row", scatter_dimension=0, tiled=True)

        t_four = t_rows.reshape(n_occ, n_virt, n_virt)
        lhs_d = t_four.transpose(1, 0, 2).reshape(n_virt, n_occ * n_virt)
        lhs_x = t_four.reshape(n_occ * n_virt, n_virt)
        out_d = jnp.dot(lhs_d, wd_blk, preferred_element_type=f32).reshape(n_virt, occ_col, n_virt)
        out_x = lax.dot_general(lhs_x, wx_blk, (((0,), (0,)), ((), ())), preferred_element_type=f32).reshape(n_virt, occ_col, n_virt)
        s_ab = out_d - out_x.transpose(2, 1, 0)
        s_ba = s_ab.transpose(2, 1, 0)
        pair = jnp.stack([s_ab.transpose(1, 0, 2), s_ba.transpose(1, 0, 2)])
        pair = pair.reshape(2, occ_col, n_col, virt_col * n_virt)
        pair = lax.all_to_all(pair, "col", 2, 1, tiled=True).reshape(2, n_occ, cols_dev)
        swapped = lax.all_to_all(pair[1], "row", 0, 0, tiled=True)
        ph_sym = pair[0] + swapped
        residual = oovv_blk.astype(f32) + ladder_sum + ph_sym
        return residual / d_blk

    return jax.shard_map(local_sweep, mesh=mesh, in_specs=(amp_spec, amp_spec, amp_spec, amp_spec, P(), wide_spec, wide_spec), out_specs=amp_spec, check_vma=False)
```

time: 374 us -> 333 us (0.89)
  local copies, waits for them, and re-layouts: 104 us -> 64.6 us
  matrix products: 67.7 us -> 40.5 us
  waiting for transfers between devices: 108 us -> 132 us
  blocking collectives: 60 us -> 66.8 us
  other arithmetic: 10.6 us -> 6.7 us
    reshape x4 -> x2, local copies, waits for them, and re-layouts: 71.1 us -> 10.1 us  [the longest x1 5.18 us: local_sweep(): t_four = t_rows.reshape(n_occ, n_virt, n_virt)]
    reduce_scatter x0 -> x1, waiting for transfers between devices: none -> 59.4 us  [local_sweep(): x_own = lax.psum_scatter(x_part, 'row', scatter_dimension=0, tiled=True)]
    all_gather x1 -> x0, waiting for transfers between devices: 56.6 us -> none  [local_sweep(): t_cols = lax.all_gather(t_half, 'row', axis=0, tiled=True)]
    reduce_scatter x1, waiting for transfers between devices: 0.02 us -> 29 us  [local_sweep(): lax.psum_scatter(ladder_part + hole_part, 'row', scatter_dimension=0, til...]
    all_to_all x1, waiting for transfers between devices: 0.01 us -> 28.4 us  [local_sweep(): lax.all_to_all(both.reshape(rows_dev + occ_col, n_row, c_dev), 'row', 1,...]
    psum x1 -> x0, waiting for transfers between devices: 25.6 us -> none  [local_sweep(): x_rows = lax.psum(x_part, 'col')]
    unnamed x13 -> x19, local copies, waits for them, and re-layouts: 8.89 us -> 34.1 us
    dot_general x4, matrix products: 50.3 us -> 26.7 us  [the longest x1 16.1 us: local_sweep(): ladder_part = jnp.dot(t_ladder, vvvv_blk, preferred_element_type=f32)]
  transfers between devices with their start and end apart: 5 -> 4, of which waited for: 3 -> 4; matrix products, arithmetic and copies ran while one was open for 42% -> 24% of each run, Pallas kernels for 0% -> 0%
where the time goes in v1:
time: 333 us; the launch traced here: 331 us
  waiting for transfers between devices  132 us (40%)
  blocking collectives  66.8 us (20%)
  local copies, waits for them, and re-layouts  64.6 us (19%)
  matrix products  40.5 us (12%)
  between operations  13.3 us (4%)
  starting transfers between devices  7.35 us (2%)
  other arithmetic  6.7 us (2%)
    reduce_scatter x1, waiting for transfers between devices, local_sweep(): x_own = lax.psum_scatter(x_part, 'row', scatter_dimension=0, tiled=True)  59.4 us
    unnamed x19, local copies, waits for them, and re-layouts  34.1 us
    reduce_scatter x1, waiting for transfers between devices, local_sweep(): lax.psum_scatter(ladder_part + hole_part, 'row', scatter_dimension=0, til...  29 us
    all_to_all x1, waiting for transfers between devices, local_sweep(): lax.all_to_all(both.reshape(rows_dev + occ_col, n_row, c_dev), 'row', 1,...  28.4 us
    all_to_all x1, blocking collectives, local_sweep(): swapped = lax.all_to_all(pair[1], 'row', 0, 0, tiled=True)  25.5 us
    all_to_all x1, blocking collectives, local_sweep(): lax.all_to_all(pair, 'col', 2, 1, tiled=True).reshape(2, n_occ, cols_dev)  17.3 us
    dot_general x1, matrix products, local_sweep(): ladder_part = jnp.dot(t_ladder, vvvv_blk, preferred_element_type=f32)  16.1 us
    all_gather x1, waiting for transfers between devices, local_sweep(): t_rows = lax.all_gather(t_half, 'col', axis=1, tiled=True)  15.2 us
  transfers between devices with their start and end apart: 4, of which 4 were waited for; matrix products, arithmetic and copies ran while one was open for 24% of the time, Pallas kernels for 0%

profile of v1, /device:TPU:0, one launch (start us, length us, event | category | flops | bytes accessed | tf_op | source)
XLA Modules:
  0.0 331.3 jit_solution(15516999055895703255)
XLA Ops:
  6.5 1.9 convert_bitcast_fusion
  8.4 0.0 all-gather.3.cloned.1.call-update
  8.4 11.7 %all_to_all.58 = bf16[4,8,5184]{2,1,0:T(8,128)(2,1)S(1)} all-to-all(bf16[4,8,5184]{2,1,0:T(8,128)(2,1)} %bitcast.74), channel_id=1, replica_groups=mesh['col'=4,'row'=32] {'col'}, dimensions={0} | all-to-all | bytes 663552 | tf_op jit(solution)/shard_map/all_to_all | solution.py:25
  20.1 0.1 copy.27
  20.3 0.7 concatenate.10
  21.0 0.2 copy.29
  21.2 15.2 %all-gather.3.cloned.1.call-done = bf16[4,5184,32]{1,2,0:T(8,128)(2,1)} async-done(((bf16[1,5184,32]{1,2,0:T(8,128)(2,1)}), bf16[4,5184,32]{1,2,0:T(8,128)(2,1)}) %all-gather.3.cloned.1.call-update) | async-done | bytes 1327120 | tf_op jit(solution)/shard_map/all_gather | solution.py:24
  36.4 2.0 copy.26
  38.4 1.1 reshape.47
  39.5 3.7 %concatenate.9 = bf16[32,32,648]{2,1,0:T(8,128)(2,1)S(1)} reshape(bf16[32,20736]{1,0:T(8,128)(2,1)S(1)} %bitcast.60) | data formatting | bytes 2654208 | tf_op jit(solution)/shard_map/concatenate | solution.py:26
  43.3 0.9 copy.28
  44.2 1.5 pad_maximum_fusion
  45.7 7.3 %all-to-all-start.1 = ((bf16[40,32,648]{2,0,1:T(8,128)(2,1)}), bf16[40,32,648]{2,0,1:T(8,128)(2,1)S(1)}, u32[]{:S(2)}, u32[]{:S(2)}) async-start(bf16[40,32,648]{2,0,1:T(8,128)(2,1)} %pad_maximum_fusion), calls=%async_computation.1 | async-start | bytes 3932160 | tf_op jit(solution)/shard_map/all_to_all | solution.py:27
  52.9 0.0 reduce-scatter.3.cloned.1.call-start
  53.0 28.4 %all-to-all-done.1 = bf16[40,32,648]{2,0,1:T(8,128)(2,1)S(1)} async-done(((bf16[40,32,648]{2,0,1:T(8,128)(2,1)}), bf16[40,32,648]{2,0,1:T(8,128)(2,1)S(1)}, u32[]{:S(2)}, u32[]{:S(2)}) %all-to-all-start.1) | async-done | bytes 1658912 | tf_op jit(solution)/shard_map/all_to_all | solution.py:27
  81.4 0.2 slice.18
  81.6 1.2 copy-done
  82.8 1.6 fusion.5
  84.4 0.0 reduce-scatter.3.cloned.1.call-update
  84.4 0.0 copy-start.1
  84.4 0.0 reduce-scatter.5.cloned.1.call-start
  84.5 16.1 %fusion.7 = f32[1024,5184]{1,0:T(8,128)} fusion(bf16[1024,648]{1,0:T(8,128)(2,1)} %bitcast.71, bf16[648,5184]{1,0:T(8,128)(2,1)} %param.10), kind=kOutput, calls=%fused_computation.17 | convolution fusion | flops 6879707136 | bytes 29279232 | tf_op jit(solution)/shard_map/dot_general | solution.py:37
  100.6 59.4 %reduce-scatter.3.cloned.1.call-done = f32[8,1024]{1,0:T(8,128)} async-done(((f32[256,1024]{1,0:T(8,128)}), f32[8,1024]{1,0:T(8,128)}) %reduce-scatter.3.cloned.1.call-update) | async-done | bytes 32784 | tf_op jit(solution)/shard_map/reduce_scatter | solution.py:32
  160.0 0.8 add_convert_fusion
  160.7 12.4 %all_gather.7 = bf16[32,1024]{1,0:T(8,128)(2,1)S(1)} all-gather(bf16[8,1024]{1,0:T(8,128)(2,1)S(1)} %add_convert_fusion), channel_id=1, replica_groups=mesh['col'=4,'row'=32] {'col'}, dimensions={0}, use_global_device_ids=true | all-gather | bytes 81920 | tf_op jit(solution)/shard_map/all_gather | solution.py:36
  173.1 13.8 %convolution_add_fusion = f32[1024,5184]{1,0:T(8,128)} fusion(f32[1024,5184]{1,0:T(8,128)} %fusion.7, bf16[32,1024]{1,0:T(8,128)(2,1)S(1)} %all_gather.7, f32[32,5184]{1,0:T(8,128)S(1)} %copy-done.1), kind=kOutput, calls=%fused_computation | convolution fusion | flops 345212928 | bytes 43196416 | tf_op jit(solution)/shard_map/dot_general | solution.py:38
  186.9 0.0 reduce-scatter.5.cloned.1.call-update
  186.9 15.3 %copy.31 = bf16[4608,1152]{0,1:T(8,128)(2,1)} copy(bf16[4608,1152]{1,0:T(8,128)(2,1)} %param.12) | data formatting | bytes 21233664 | tf_op args[5]
  202.3 15.3 %copy.32 = bf16[4608,1152]{0,1:T(8,128)(2,1)} copy(bf16[4608,1152]{1,0:T(8,128)(2,1)} %param.13) | data formatting | bytes 21233664 | tf_op args[6]
  217.6 5.2 %reshape.44 = bf16[32,144,144]{2,1,0:T(8,128)(2,1)} reshape(bf16[32,20736]{1,0:T(8,128)(2,1)S(1)} %bitcast.61) | data formatting | bytes 2654208 | tf_op jit(solution)/shard_map/reshape | solution.py:41
  222.8 5.1 %reshape_reshape.3 = bf16[4608,144]{1,0:T(8,128)(2,1)} reshape(bf16[32,20736]{1,0:T(8,128)(2,1)S(1)} %bitcast.62) | data formatting | bytes 2654208 | tf_op jit(solution)/shard_map/reshape;reshape | solution.py:43
  227.9 3.9 %copy.30 = bf16[144,32,144]{2,1,0:T(8,128)(2,1)} copy(bf16[144,32,144]{2,0,1:T(8,128)(2,1)} %bitcast.67) | data formatting | bytes 2654208 | tf_op jit(solution)/shard_map/transpose | solution.py:42
  231.8 4.9 %reshape.48 = bf16[144,4608,1]{1,0,2:T(8,128)(2,1)S(1)} reshape(bf16[144,32,144]{2,1,0:T(8,128)(2,1)} %copy.30) | data formatting | bytes 2654208 | tf_op jit(solution)/shard_map/reshape | solution.py:42
  236.7 6.0 %fusion.8 = f32[144,8,144]{2,0,1:T(8,128)S(1)} fusion(bf16[144,4608,1]{1,0,2:T(8,128)(2,1)S(1)} %reshape.48, bf16[8,144,4608]{2,1,0:T(8,128)(2,1)} %bitcast.66), kind=kOutput, calls=%fused_computation.18 | convolution fusion | flops 1528823808 | bytes 12607488 | tf_op jit(solution)/shard_map/dot_general | solution.py:44
  242.7 0.5 slice-done.2
  243.2 0.7 copy-done.2
  243.9 3.0 bitcast_subtract_fusion
  246.9 0.2 bitcast_subtract_fusion.1
  247.1 1.1 stack.9
  248.1 0.6 copy.36
  248.7 1.1 stack.10
  249.8 0.3 pad_maximum_fusion.1
  250.1 0.1 copy.37
  250.2 17.3 %all_to_all.59 = f32[2,8,4,5184]{3,1,0,2:T(8,128)S(1)} all-to-all(f32[2,8,4,5184]{3,1,0,2:T(8,128)S(1)} %copy.37), channel_id=1, replica_groups=mesh['col'=4,'row'=32] {'col'}, dimensions={2} | all-to-all | bytes 2654208 | tf_op jit(solution)/shard_map/all_to_all | solution.py:50
  267.5 0.7 copy.38
  268.2 25.5 %all_to_all.60 = f32[32,1,5184]{2,1,0:T(1,128)S(1)} all-to-all(f32[32,1,5184]{2,1,0:T(1,128)S(1)} %copy.38), channel_id=1, replica_groups=mesh['col'=4,'row'=32] {'row'}, dimensions={0} | all-to-all | bytes 1327104 | tf_op jit(solution)/shard_map/all_to_all | solution.py:51
  293.7 29.0 %reduce-scatter.5.cloned.1.call-done = f32[32,5184]{1,0:T(8,128)} async-done(((f32[1024,5184]{1,0:T(8,128)}), f32[32,5184]{1,0:T(8,128)}) %reduce-scatter.5.cloned.1.call-update) | async-done | bytes 663568 | tf_op jit(solution)/shard_map/reduce_scatter | solution.py:39
  322.7 2.1 fusion.4
  (15 shorter events, 0.1 us)
Async XLA Ops:
  6.5 29.9 %all-gather.3.cloned.1.call-start = ((), (), s32[]{:S(2)}) async-start(), calls=%async_computation.8 | async-start | bytes 1679360 | tf_op jit(solution)/shard_map/all_gather | solution.py:24
  45.7 35.7 %all-to-all-start.1 = ((bf16[40,32,648]{2,0,1:T(8,128)(2,1)}), bf16[40,32,648]{2,0,1:T(8,128)(2,1)S(1)}, u32[]{:S(2)}, u32[]{:S(2)}) async-start(bf16[40,32,648]{2,0,1:T(8,128)(2,1)} %pad_maximum_fusion), calls=%async_computation.1 | async-start | bytes 3932160 | tf_op jit(solution)/shard_map/all_to_all | solution.py:27
  52.9 107.0 %reduce-scatter.3.cloned.1.call-start = ((), (), s32[]{:S(2)}) async-start(), calls=%async_computation.6 | async-start | bytes 1081344 | tf_op jit(solution)/shard_map/reduce_scatter | solution.py:32
  81.6 1.2 copy-start
  84.4 88.7 %copy-start.1 = (f32[32,5184]{1,0:T(8,128)S(1)}, f32[32,5184]{1,0:T(8,128)}, u32[]{:S(2)}) copy-start(f32[32,5184]{1,0:T(8,128)} %param.7) | copy-start | bytes 1990660
  84.4 238.3 %reduce-scatter.5.cloned.1.call-start = ((), (), s32[]{:S(2)}) async-start(), calls=%async_computation.7 | async-start | bytes 22167552 | tf_op jit(solution)/shard_map/reduce_scatter | solution.py:39
  231.8 11.0 %slice-start = ((s8[10616832]{0:T(1024)(128)(4,1)}), s8[2228224]{0:T(1024)(128)(4,1)S(1)}, s32[]{:S(2)}) async-start(s8[10616832]{0:T(1024)(128)(4,1)} %bitcast.63), calls=%async_computation.9 | async-start | bytes 4456448
  236.7 6.1 %slice-start.1 = ((s8[10616832]{0:T(1024)(128)(4,1)}), s8[4194304]{0:T(1024)(128)(4,1)S(1)}, s32[]{:S(2)}) async-start(s8[10616832]{0:T(1024)(128)(4,1)} %bitcast.63), calls=%async_computation.10 | async-start | bytes 8388608
  236.7 6.5 %slice-start.2 = ((s8[10616832]{0:T(1024)(128)(4,1)}), s8[4194304]{0:T(1024)(128)(4,1)S(1)}, s32[]{:S(2)}) async-start(s8[10616832]{0:T(1024)(128)(4,1)} %bitcast.63), calls=%async_computation.11 | async-start | bytes 8388608
  236.7 7.2 %copy-start.2 = (bf16[4608,144]{1,0:T(8,128)(2,1)S(1)}, bf16[4608,144]{1,0:T(8,128)(2,1)}, u32[]{:S(2)}) copy-start(bf16[4608,144]{1,0:T(8,128)(2,1)} %reshape_reshape.3) | copy-start | bytes 3981316
  267.5 55.2 %copy-start.3 = (bf16[32,5184]{1,0:T(8,128)(2,1)S(1)}, bf16[32,5184]{1,0:T(8,128)(2,1)}, u32[]{:S(2)}) copy-start(bf16[32,5184]{1,0:T(8,128)(2,1)} %param.9) | copy-start | bytes 995332
  267.5 55.2 %copy-start.4 = (f32[32,5184]{1,0:T(8,128)S(1)}, f32[32,5184]{1,0:T(8,128)}, u32[]{:S(2)}) copy-start(f32[32,5184]{1,0:T(8,128)} %param.8) | copy-start | bytes 1990660
Sparse Core Ops, SparseCore 0:
  9.0 27.3 all-gather.2
  84.5 75.4 reduce-scatter.2
  187.0 135.5 reduce-scatter.4

commit v2 on v1

v2 whole, which is shorter than its diff:
```python
import functools
import math
import jax
import jax.numpy as jnp
from jax import lax
from jax.experimental import pallas as pl
from jax.experimental.pallas import tpu as pltpu
from jax.sharding import PartitionSpec as P

MESH = pl.DeviceIdType.MESH
BF16 = jnp.bfloat16
F32 = jnp.float32
VMEM_LIMIT = 66 * 1000 * 1000


def _place():
    x = lax.axis_index("col")
    r = lax.axis_index("row")
    core = r % 2
    q = r // 2
    return x, q // 4, q % 4, core, q


def _rc(src, dst, ssem, rsem, dev):
    return pltpu.make_async_remote_copy(src_ref=src, dst_ref=dst, send_sem=ssem, recv_sem=rsem, device_id=dev, device_id_type=MESH)


def gather_kernel(ts, t2, vs, tl, vl, tr, g, g_s, g_r, t_s, t_r, p_s, p_r, v_s, v_r, f_s, f_r, loc):
    x, z, y, core, q = _place()
    r = lax.axis_index("row")
    right, left = (x + 1) % 4, (x + 3) % 4
    half = ts.shape[0] // 2
    hrow = t2.shape[0] // 2

    own = pltpu.make_async_copy(ts, g.at[x], loc.at[0])
    own.start()
    ag_r = _rc(ts, g.at[x], g_s.at[0], g_r.at[0], (right, r))
    ag_l = _rc(ts, g.at[x], g_s.at[1], g_r.at[1], (left, r))
    ag_r.start()
    ag_l.start()
    own2 = pltpu.make_async_copy(t2, tr.at[x], loc.at[2])
    own2.start()

    def v_copy(x2, yd):
        return _rc(vs.at[pl.ds(2 * yd, 2), x2], vl.at[:, core, q], v_s.at[x2, yd], v_r.at[q], (x2, (x * 4 + yd) * 2 + core))

    def v_each(fn_remote, fn_local):
        for i in range(4):
            for k in range(4):
                x2, yd = (x + i) % 4, (y + k) % 4
                if i == 0 and k == 0:
                    mine = x == z

                    @pl.when(mine)
                    def _():
                        fn_local(x2, yd)

                    @pl.when(jnp.logical_not(mine))
                    def _():
                        fn_remote(x2, yd)
                else:
                    fn_remote(x2, yd)

    own.wait()

    def t_copy(xs, yd):
        return _rc(g.at[xs, pl.ds(2 * yd, 2)], tl.at[:, q], t_s.at[xs, yd], t_r.at[q], (x, (xs * 4 + yd) * 2 + core))

    def t_block(rel):
        xs = (x + rel) % 4
        for k in range(4):
            yd = (y + k) % 4
            if k == 0:
                mine = xs == z

                @pl.when(mine)
                def _():
                    pltpu.make_async_copy(g.at[xs, pl.ds(2 * yd, 2)], tl.at[:, q], loc.at[1]).start()

                @pl.when(jnp.logical_not(mine))
                def _():
                    t_copy(xs, yd).start()
            else:
                t_copy(xs, yd).start()

    t_block(0)
    v_each(lambda a, b: v_copy(a, b).start(),
           lambda a, b: pltpu.make_async_copy(vs.at[pl.ds(2 * b, 2), a], vl.at[:, core, q], loc.at[3]).start())
    ag_r.wait_recv()
    fw_r = _rc(g.at[left, pl.ds(0, half)], g.at[left, pl.ds(0, half)], g_s.at[2], g_r.at[2], (right, r))
    fw_r.start()
    t_block(3)
    ag_l.wait_recv()
    fw_l = _rc(g.at[right, pl.ds(half, half)], g.at[right, pl.ds(half, half)], g_s.at[3], g_r.at[3], (left, r))
    fw_l.start()
    t_block(1)
    own2.wait()
    p_r0 = _rc(t2, tr.at[x], p_s.at[0], p_r.at[0], (right, r))
    p_l0 = _rc(t2, tr.at[x], p_s.at[1], p_r.at[1], (left, r))
    p_r0.start()
    p_l0.start()
    fw_r.wait_recv()
    fw_l.wait_recv()
    t_block(2)
    p_r0.wait_recv()
    pf_r = _rc(tr.at[left, pl.ds(0, hrow)], tr.at[left, pl.ds(0, hrow)], p_s.at[2], p_r.at[2], (right, r))
    pf_r.start()
    p_l0.wait_recv()
    pf_l = _rc(tr.at[right, pl.ds(hrow, hrow)], tr.at[right, pl.ds(hrow, hrow)], p_s.at[3], p_r.at[3], (left, r))
    pf_l.start()

    for k in range(16):
        qs = (q + k) % 16
        if k == 0:
            @pl.when(x == z)
            def _():
                pltpu.make_async_copy(vs.at[pl.ds(2 * y, 2), x], vl.at[:, core, q], loc.at[3]).wait()

            @pl.when(x != z)
            def _():
                _rc(vs.at[pl.ds(2 * y, 2), x], vl.at[:, core, qs], v_s.at[x, y], v_r.at[qs], (x, r)).wait_recv()
        else:
            _rc(vs.at[pl.ds(2 * y, 2), x], vl.at[:, core, qs], v_s.at[x, y], v_r.at[qs], (x, r)).wait_recv()
    fwd = _rc(vl.at[:, core], vl.at[:, core], f_s, f_r, (x, q * 2 + 1 - core))
    fwd.start()
    for k in range(16):
        qs = (q + k) % 16
        if k == 0:
            pltpu.make_async_copy(g.at[x, pl.ds(2 * y, 2)], tl.at[:, q], loc.at[1]).wait()
        else:
            _rc(g.at[x, pl.ds(2 * y, 2)], tl.at[:, qs], t_s.at[x, y], t_r.at[qs], (x, r)).wait_recv()
    fwd.wait()
    pf_r.wait_recv()
    pf_l.wait_recv()
    for c in (ag_r, ag_l, fw_r, fw_l, p_r0, p_l0, pf_r, pf_l):
        c.wait_send()
    for rel in range(4):
        xs = (x + rel) % 4
        for k in range(4):
            yd = (y + k) % 4
            if k == 0:
                @pl.when(xs != z)
                def _():
                    t_copy(xs, yd).wait_send()
            else:
                t_copy(xs, yd).wait_send()
    v_each(lambda a, b: v_copy(a, b).wait_send(), lambda a, b: None)


def gather_call(ts, t2, vs):
    n_p, rows, cw = ts.shape
    cols = t2.shape[1]
    dma = pltpu.SemaphoreType.DMA
    vm = pl.BlockSpec(memory_space=pltpu.VMEM)
    return pl.pallas_call(
        gather_kernel,
        out_shape=[
            jax.ShapeDtypeStruct((2, 16, rows, cw), BF16),
            jax.ShapeDtypeStruct((2, 2, 16, rows // 4, cw), BF16),
            jax.ShapeDtypeStruct((4, rows, cols), BF16),
        ],
        in_specs=[vm, vm, vm],
        out_specs=[vm, vm, vm],
        scratch_shapes=[
            pltpu.VMEM((4, n_p, rows, cw), BF16),
            dma((4,)), dma((4,)), dma((4, 4)), dma((16,)), dma((4,)), dma((4,)), dma((4, 4)), dma((16,)), dma, dma, dma((4,)),
        ],
        compiler_params=pltpu.CompilerParams(has_side_effects=True, vmem_limit_bytes=VMEM_LIMIT),
        name="gather",
    )(ts, t2, vs)


N_CH = 10
CW = 512
TAIL = 64


def ladder_kernel(tl, vl, v_hbm, t2, oo, out, v_buf, t_pair, m_t, x_part, x_in, m_all, p_b, p_t, r1, r1t, r2, r2t, qb, qt,
                  vl_s, vx_s, vx_r, tp_s, tp_r, x_s, x_r, m_s, m_r, s1, w1, s2, w2):
    x, z, y, core, q = _place()
    r = lax.axis_index("row")
    mate = (x, q * 2 + 1 - core)
    mcore = 1 - core
    n_c = v_hbm.shape[0]
    n_v = 9
    cols = [(i * 640, 640) for i in range(8)] + [(5120, 64)]

    v_in = []
    v_x = []
    for i, (c0, w) in enumerate(cols):
        a = pltpu.make_async_copy(v_hbm.at[:, pl.ds(c0, w)], v_buf.at[core, :, pl.ds(c0, w)], vl_s.at[i])
        b = _rc(v_hbm.at[:, pl.ds(c0, w)], v_buf.at[core, :, pl.ds(c0, w)], vx_s.at[i], vx_r.at[i], mate)
        a.start()
        b.start()
        v_in.append(a)
        v_x.append(b)
    tp_l = pltpu.make_async_copy(t2, t_pair.at[core], tp_s.at[0])
    tp_x = _rc(t2, t_pair.at[core], tp_s.at[1], tp_r, mate)
    tp_l.start()
    tp_x.start()

    rows = tl.shape[2]
    k8 = vl.shape[3]
    n_i = 16 * rows
    n_k = 32 * k8
    tl0 = tl[0].reshape(n_i, n_c)
    tl1 = tl[1].reshape(n_i, n_c)
    dn = (((1,), (1,)), ((), ()))
    xp = lax.dot_general(vl[0].reshape(n_k, n_c), tl0, dn, preferred_element_type=F32)
    xp = xp + lax.dot_general(vl[1].reshape(n_k, n_c), tl1, dn, preferred_element_type=F32)
    x_part[...] = xp.reshape(2, 16, k8, n_i)

    def x_copy(k):
        qd = (q + k) % 16
        return _rc(x_part.at[:, qd], x_in.at[q], x_s.at[k], x_r.at[k], (x, qd * 2 + core))

    for k in range(1, 16):
        x_copy(k).start()
    x_in[q] = x_part[:, q]
    for k in range(1, 16):
        x_copy(k).wait_recv()
    xs = x_in[0]
    for k in range(1, 16):
        xs = xs + x_in[k]
    m_all[x] = (oo[...].astype(F32) + 0.5 * xs).astype(BF16)

    def m_copy(k):
        return _rc(m_all.at[x], m_all.at[x], m_s.at[k], m_r.at[k], ((x + k) % 4, r))

    for k in range(1, 4):
        m_copy(k).start()
    tp_l.wait()
    tp_x.wait()
    for i in range(n_v):
        v_in[i].wait()
        v_x[i].wait()
    for k in range(1, 4):
        m_copy(k).wait_recv()
    mf = m_all[...].astype(F32)
    m_t[...] = jnp.concatenate([mf[xx, cc] for cc in range(2) for xx in range(4)], axis=0).T.astype(BF16)

    def coords(a):
        return y * a + z * (1 - a), z * a + y * (1 - a)

    def to1(a, d):
        yy = (y + d * a) % 4
        zz = (z + d * (1 - a)) % 4
        return (x, (zz * 4 + yy) * 2 + core)

    def to2(a, d):
        yy = (y + d * (1 - a)) % 4
        zz = (z + d * a) % 4
        return (x, (zz * 4 + yy) * 2 + core)

    def phase1(t, a, pb, rb):
        u, _ = coords(a)
        lo, hi = pl.ds(0, 2), pl.ds(2, 2)
        far, up, dn_ = (u + 2) % 4, (u + 1) % 4, (u + 3) % 4

        def mk(i, src, d):
            return _rc(pb.at[src], rb.at[i], s1.at[t, i], w1.at[t, i], to1(a, d))
        args = ((far, lo), 1), ((far, hi), 3), ((up, hi), 1), ((dn_, lo), 3), ((up, lo), 1), ((dn_, hi), 3)
        return lambda i: mk(i, *args[i])

    def phase2(t, a, pb, rb):
        u, v = coords(a)
        h = rows // 2
        lo, hi = pl.ds(0, h), pl.ds(h, h)
        far, up, dn_ = (v + 2) % 4, (v + 1) % 4, (v + 3) % 4

        def mk(i, src, d):
            return _rc(pb.at[src], rb.at[i], s2.at[t, i], w2.at[t, i], to2(a, d))
        args = ((u, far, lo), 1), ((u, far, hi), 3), ((u, up, hi), 1), ((u, dn_, lo), 3), ((u, up, lo), 1), ((u, dn_, hi), 3)
        return lambda i: mk(i, *args[i])

    def bufs(t):
        return p_b.at[t], r1.at[t], r2.at[t]

    def compute(t, a, pb, c0, w):
        vb0 = v_buf[0, :, pl.ds(c0, w)]
        vb1 = v_buf[1, :, pl.ds(c0, w)]
        tp = t_pair[:, :, pl.ds(c0, w)].reshape(2 * rows, w)
        acc = jnp.dot(tl[0].reshape(n_i, n_c), vb0, preferred_element_type=F32)
        acc = acc + jnp.dot(tl[1].reshape(n_i, n_c), vb1, preferred_element_type=F32)
        acc = acc + jnp.dot(m_t[...], tp, preferred_element_type=F32)
        for zb in range(4):
            for yb in range(4):
                b = zb * 4 + yb
                pb[yb * a + zb * (1 - a), zb * a + yb * (1 - a)] = acc[b * rows:(b + 1) * rows]

    def l1(t, a, pb, rb, c0, w):
        compute(t, a, pb, c0, w)
        cs = phase1(t, a, pb, rb)
        for i in range(4):
            cs(i).start()

    def l2(t, a, pb, rb):
        u, _ = coords(a)
        cs = phase1(t, a, pb, rb)
        up, dn_ = (u + 1) % 4, (u + 3) % 4
        cs(0).wait_recv()
        pb[up, 0:2] = pb[up, 0:2] + rb[0]
        cs(4).start()
        cs(1).wait_recv()
        pb[dn_, 2:4] = pb[dn_, 2:4] + rb[1]
        cs(5).start()

    def l3(t, a, pb, rb, rb2):
        u, _ = coords(a)
        cs = phase1(t, a, pb, rb)
        for i in (3, 2, 4, 5):
            cs(i).wait_recv()
        pb[u, 0:2] = pb[u, 0:2] + rb[4] + rb[3]
        pb[u, 2:4] = pb[u, 2:4] + rb[2] + rb[5]
        cs = phase2(t, a, pb, rb2)
        for i in range(4):
            cs(i).start()

    def l4(t, a, pb, rb2):
        u, v = coords(a)
        h = rows // 2
        cs = phase2(t, a, pb, rb2)
        up, dn_ = (v + 1) % 4, (v + 3) % 4
        cs(0).wait_recv()
        pb[u, up, 0:h] = pb[u, up, 0:h] + rb2[0]
        cs(4).start()
        cs(1).wait_recv()
        pb[u, dn_, h:rows] = pb[u, dn_, h:rows] + rb2[1]
        cs(5).start()

    def l5(t, a, pb, rb, rb2, c0, w):
        u, v = coords(a)
        h = rows // 2
        cs = phase2(t, a, pb, rb2)
        for i in (2, 3, 4, 5):
            cs(i).wait_recv()
        out[0:h, pl.ds(c0, w)] = pb[u, v, 0:h] + rb2[4] + rb2[3]
        out[h:rows, pl.ds(c0, w)] = pb[u, v, h:rows] + rb2[2] + rb2[5]
        ds = phase1(t, a, pb, rb)
        for i in range(6):
            cs(i).wait_send()
            ds(i).wait_send()

    def kind(t):
        return 1 - t % 2

    def col0(t):
        return pl.multiple_of((t // 2) * CW + (t % 2) * (N_CH // 2) * CW, 128)

    ct = N_CH * CW
    l1(N_CH, 1, p_t, r1t, ct, TAIL)

    def f1(t, c):
        pb, rb, _ = bufs(t)
        l1(t, kind(t), pb, rb, col0(t), CW)
        return c
    lax.fori_loop(0, N_CH, f1, 0)
    l2(N_CH, 1, p_t, r1t)

    def f2(t, c):
        pb, rb, _ = bufs(t)
        l2(t, kind(t), pb, rb)
        return c
    lax.fori_loop(0, N_CH, f2, 0)
    l3(N_CH, 1, p_t, r1t, r2t)
    l4(N_CH, 1, p_t, r2t)
    pb, rb, rb2 = bufs(0)
    l3(0, 1, pb, rb, rb2)

    def f3(t, c):
        pb, rb, rb2 = bufs(t)
        l3(t, kind(t), pb, rb, rb2)
        pb, rb, rb2 = bufs(t - 1)
        l4(t - 1, kind(t - 1), pb, rb2)
        return c
    lax.fori_loop(1, N_CH, f3, 0)
    pb, rb, rb2 = bufs(N_CH - 1)
    l4(N_CH - 1, (N_CH % 2), pb, rb2)
    l5(N_CH, 1, p_t, r1t, r2t, ct, TAIL)

    def f5(t, c):
        pb, rb, rb2 = bufs(t)
        l5(t, kind(t), pb, rb, rb2, col0(t), CW)
        return c
    lax.fori_loop(0, N_CH, f5, 0)
    for k in range(1, 16):
        x_copy(k).wait_send()
    for k in range(1, 4):
        m_copy(k).wait_send()


def ladder_call(tl, vl, v, t2, oo):
    _, _, rows, n_c = tl.shape
    k8 = vl.shape[3]
    cols = t2.shape[1]
    dma = pltpu.SemaphoreType.DMA
    vm = pl.BlockSpec(memory_space=pltpu.VMEM)
    n = N_CH + 1
    return pl.pallas_call(
        ladder_kernel,
        out_shape=jax.ShapeDtypeStruct((rows, cols), F32),
        in_specs=[vm, vm, pl.BlockSpec(memory_space=pl.ANY), vm, vm],
        out_specs=vm,
        scratch_shapes=[
            pltpu.VMEM((2, n_c, cols), BF16),
            pltpu.VMEM((2, rows, cols), BF16),
            pltpu.VMEM((16 * rows, 8 * k8), BF16),
            pltpu.VMEM((2, 16, k8, 16 * rows), F32),
            pltpu.VMEM((16, 2, k8, 16 * rows), F32),
            pltpu.VMEM((4, 2, k8, 16 * rows), BF16),
            pltpu.VMEM((N_CH, 4, 4, rows, CW), F32),
            pltpu.VMEM((4, 4, rows, TAIL), F32),
            pltpu.VMEM((N_CH, 6, 2, rows, CW), F32),
            pltpu.VMEM((6, 2, rows, TAIL), F32),
            pltpu.VMEM((N_CH, 6, rows // 2, CW), F32),
            pltpu.VMEM((6, rows // 2, TAIL), F32),
            pltpu.VMEM((8, 128), F32),
            pltpu.VMEM((8, 128), F32),
            dma((9,)), dma((9,)), dma((9,)), dma((2,)), dma, dma((16,)), dma((16,)), dma((4,)), dma((4,)),
            dma((n, 6)), dma((n, 6)), dma((n, 6)), dma((n, 6)),
        ],
        compiler_params=pltpu.CompilerParams(has_side_effects=True, vmem_limit_bytes=VMEM_LIMIT),
        name="ladder",
    )(tl, vl, v, t2, oo)


def solution(mesh):
    n_row = mesh.shape["row"]
    n_col = mesh.shape["col"]
    amp_spec = P("row", "col")
    wide_spec = P(None, "col")

    def local_sweep(t_blk, d_blk, oovv_blk, vvvv_blk, oooo_full, wd_blk, wx_blk):
        rows_dev, cols_dev = t_blk.shape
        n_occ = math.isqrt(oooo_full.shape[0])
        n_virt = wd_blk.shape[0] // n_occ
        occ_col = n_occ // n_col
        virt_col = n_virt // n_col
        c_dev = vvvv_blk.shape[0]
        n_p = cols_dev // c_dev
        q = lax.axis_index("row") // 2
        core = lax.axis_index("row") % 2
        t_half = t_blk.astype(BF16)
        ts = t_half.reshape(rows_dev, n_p, c_dev).transpose(1, 0, 2)
        vs = oovv_blk.reshape(n_col, occ_col, n_p, c_dev).transpose(2, 0, 1, 3)
        tl, vl, tr = gather_call(ts, t_half, vs)
        oo = oooo_full.reshape(16, 2, n_col, occ_col, 16, 2, n_occ)
        oo = lax.dynamic_index_in_dim(oo, q, 0, False)
        oo = lax.dynamic_index_in_dim(oo, lax.axis_index("col"), 1, False)
        oo = lax.dynamic_index_in_dim(oo, core, 3, False)
        oo = oo.reshape(2, occ_col, 16 * n_occ)
        ladder_sum = ladder_call(tl, vl, vvvv_blk, t_half, oo)

        t_four = tr.reshape(n_col, n_occ, virt_col, n_virt).transpose(1, 0, 2, 3).reshape(n_occ, n_virt, n_virt)
        lhs_d = t_four.transpose(1, 0, 2).reshape(n_virt, n_occ * n_virt)
        lhs_x = t_four.reshape(n_occ * n_virt, n_virt)
        out_d = jnp.dot(lhs_d, wd_blk, preferred_element_type=F32).reshape(n_virt, occ_col, n_virt)
        out_x = lax.dot_general(lhs_x, wx_blk, (((0,), (0,)), ((), ())), preferred_element_type=F32).reshape(n_virt, occ_col, n_virt)
        s_ab = out_d - out_x.transpose(2, 1, 0)
        s_ba = s_ab.transpose(2, 1, 0)
        pair = jnp.stack([s_ab.transpose(1, 0, 2), s_ba.transpose(1, 0, 2)])
        pair = pair.reshape(2, occ_col, n_col, virt_col * n_virt)
        pair = lax.all_to_all(pair, "col", 2, 1, tiled=True).reshape(2, n_occ, cols_dev)
        swapped = lax.all_to_all(pair[1], "row", 0, 0, tiled=True)
        ph_sym = pair[0] + swapped
        residual = oovv_blk.astype(F32) + ladder_sum + ph_sym
        return residual / d_blk

    return jax.shard_map(local_sweep, mesh=mesh, in_specs=(amp_spec, amp_spec, amp_spec, amp_spec, P(), wide_spec, wide_spec), out_specs=amp_spec, check_vma=False)
```

time: 333 us -> 269 us (0.81)
  Pallas kernels: 0 us -> 151 us
  waiting for transfers between devices: 132 us -> 0.01 us
  blocking collectives: 66.8 us -> 21.4 us
  matrix products: 40.5 us -> 10.2 us
  between operations: 13.3 us -> 0.17 us
  local copies, waits for them, and re-layouts: 64.6 us -> 70.5 us
    pallas_call x0 -> x2, Pallas kernels: none -> 151 us  [the longest x1 98.3 us: ladder_call(): pl.pallas_call(ladder_kernel, out_shape=jax.ShapeDtypeStruct((rows, cols)...]
    reduce_scatter x2 -> x0, waiting for transfers between devices: 88.4 us -> none  [the longest x1 59.4 us: local_sweep(): x_own = lax.psum_scatter(x_part, 'row', scatter_dimension=0, tiled=True)]
    all_to_all x2 -> x0, blocking collectives: 37.2 us -> none  [the longest x1 25.5 us: local_sweep(): swapped = lax.all_to_all(pair[1], 'row', 0, 0, tiled=True)]
    dot_general x4 -> x1, matrix products: 37.5 us -> 5.79 us  [local_sweep(): jnp.dot(lhs_d, wd_blk, preferred_element_type=F32)]
    all_to_all x1, waiting for transfers between devices: 28.4 us -> 0.01 us  [local_sweep(): swapped = lax.all_to_all(pair[1], 'row', 0, 0, tiled=True)]
    all_gather x1 -> x0, waiting for transfers between devices: 15.2 us -> none  [local_sweep(): t_rows = lax.all_gather(t_half, 'col', axis=1, tiled=True)]
    all_gather x1 -> x0, blocking collectives: 12.4 us -> none  [local_sweep(): hole_mat = lax.all_gather(m_own, 'col', axis=0, tiled=True)]
    reshape x1 -> x7, local copies, waits for them, and re-layouts: 5.18 us -> 16.3 us  [the longest x1 7.93 us: local_sweep(): oo = oooo_full.reshape(16, 2, n_col, occ_col, 16, 2, n_occ)]
  transfers between devices with their start and end apart: 4 -> 1, of which waited for: 4 -> 0; matrix products, arithmetic and copies ran while one was open for 24% -> 4% of each run, Pallas kernels for 0% -> 37%
where the time goes in v2:
time: 269 us; the launch traced here: 268 us
  Pallas kernels  151 us (56%)
  local copies, waits for them, and re-layouts  70.5 us (26%)
  blocking collectives  21.4 us (8%)
  matrix products  10.2 us (4%)
  starting transfers between devices  9.22 us (3%)
  other arithmetic  5.41 us (2%)
    pallas_call x1, Pallas kernels, ladder_call(): pl.pallas_call(ladder_kernel, out_shape=jax.ShapeDtypeStruct((rows, cols)...  98.3 us
    pallas_call x1, Pallas kernels, gather_call(): pl.pallas_call(gather_kernel, out_shape=[jax.ShapeDtypeStruct((2, 16, row...  52.4 us
    unnamed x18, local copies, waits for them, and re-layouts  33.9 us
    all_to_all x1, blocking collectives, local_sweep(): lax.all_to_all(pair, 'col', 2, 1, tiled=True).reshape(2, n_occ, cols_dev)  21.4 us
    all_to_all x1, starting transfers between devices, local_sweep(): swapped = lax.all_to_all(pair[1], 'row', 0, 0, tiled=True)  9.22 us
    reshape x1, local copies, waits for them, and re-layouts, local_sweep(): oo = oooo_full.reshape(16, 2, n_col, occ_col, 16, 2, n_occ)  7.93 us
    dot_general x1, matrix products, local_sweep(): jnp.dot(lhs_d, wd_blk, preferred_element_type=F32)  5.79 us
  transfers between devices with their start and end apart: 1, of which 0 were waited for; matrix products, arithmetic and copies ran while one was open for 4% of the time, Pallas kernels for 37%

profile of v2, /device:TPU:0, one launch (start us, length us, event | category | flops | bytes accessed | tf_op | source)
XLA Modules:
  0.0 267.5 jit_solution(14810573649552132983)
XLA Ops:
  0.0 0.0 copy-start.6
  0.0 1.2 convert_element_type.7.t2
  1.2 0.0 copy-start.2
  1.2 0.7 reshape.44
  1.9 0.8 copy.51
  2.7 0.0 copy-done.6
  2.7 0.7 reshape.45
  3.4 0.8 copy.50
  4.3 0.0 copy-done.2
  4.3 52.4 %gather.1 = (bf16[2,16,32,648]{3,2,1,0:T(8,128)(2,1)}, bf16[2,2,16,8,648]{4,3,2,1,0:T(8,128)(2,1)}, bf16[4,32,5184]{2,1,0:T(8,128)(2,1)}) custom-call(bf16[8,32,648]{2,1,0:T(8,128)(2,1)} %bitcast.52, bf16[32,5184]{1,0:T(8,128)(2,1)} %copy-done.2, bf16[8,4,8,648]{3,2,1,0:T(8,128)(2,1)} %bitcast.53), custom_call_target="tpu_custom_call" | custom-call | tf_op jit(solution)/shard_map/gather/pallas_call | solution.py:155
  56.7 4.6 %reshape.48 = bf16[4,32,36,144]{3,2,1,0:T(8,128)(2,1)S(1)} reshape(bf16[4,32,5184]{2,1,0:T(8,128)(2,1)} %get-tuple-element.10) | data formatting | bytes 2654208 | tf_op jit(solution)/shard_map/reshape | solution.py:454
  61.4 2.0 copy.32
  63.4 1.8 copy.34
  65.2 0.0 copy-start.1
  65.2 5.2 %reshape.56 = bf16[4608,144,1]{1,0,2:T(8,128)(2,1)} reshape(bf16[32,4,36,144]{3,2,1,0:T(8,128)(2,1)} %copy.34) | data formatting | bytes 2654208 | tf_op jit(solution)/shard_map/reshape;reshape | solution.py:456
  70.4 0.0 copy-done.1
  70.4 4.2 %reshape.51 = bf16[144,4608,1]{1,0,2:T(8,128)(2,1)} reshape(bf16[144,32,144]{2,1,0:T(8,128)(2,1)S(1)} %bitcast.49) | data formatting | bytes 2654208 | tf_op jit(solution)/shard_map/reshape | solution.py:455
  74.6 15.3 %copy.33 = bf16[4608,1152]{0,1:T(8,128)(2,1)} copy(bf16[4608,1152]{1,0:T(8,128)(2,1)} %param.12) | data formatting | bytes 21233664 | tf_op args[5]
  90.0 0.0 copy-start.7
  90.0 15.4 %copy.35 = bf16[4608,1152]{0,1:T(8,128)(2,1)} copy(bf16[4608,1152]{1,0:T(8,128)(2,1)} %param.13) | data formatting | bytes 21233664 | tf_op args[6]
  105.4 0.0 copy-done.7
  105.4 0.0 copy-start
  105.4 0.0 copy-start.4
  105.4 5.8 %fusion.3 = f32[144,8,144]{2,0,1:T(8,128)S(1)} fusion(bf16[144,4608,1]{1,0,2:T(8,128)(2,1)S(1)} %copy-done.7, bf16[8,144,4608]{2,1,0:T(8,128)(2,1)} %bitcast.48), kind=kOutput, calls=%fused_computation.11 | convolution fusion | flops 1528823808 | bytes 12607488 | tf_op jit(solution)/shard_map/dot_general | solution.py:457
  111.2 1.3 copy-done
  112.5 0.7 copy-done.4
  113.1 4.4 %bitcast_subtract_fusion = (f32[8,144,144]{1,2,0:T(8,128)}, f32[144,8,144]{0,2,1:T(8,128)}) fusion(f32[144,8,144]{2,0,1:T(8,128)S(1)} %fusion.3, bf16[4608,144,1]{1,0,2:T(8,128)(2,1)S(1)} %copy-done.4, bf16[8,144,4608]{2,1,0:T(8,128)(2,1)S(1)} %bitcast.47), kind=kOutput, calls=%fused_computation.1 | convolution fusion | flops 1528989696 | bytes 13934592 | tf_op jit(solution)/shard_map/dot_general | solution.py:458
  117.5 1.8 copy.39
  119.4 1.1 stack.10
  120.4 1.4 bitcast_subtract_fusion.1
  121.8 1.1 stack.9
  122.9 0.3 pad_maximum_fusion
  123.2 0.1 copy.40
  123.3 21.4 %all_to_all.27 = f32[2,8,4,5184]{3,1,0,2:T(8,128)S(1)} all-to-all(f32[2,8,4,5184]{3,1,0,2:T(8,128)S(1)} %copy.40), channel_id=1, replica_groups=mesh['col'=4,'row'=32] {'col'}, dimensions={2} | all-to-all | bytes 2654208 | tf_op jit(solution)/shard_map/all_to_all | solution.py:463
  144.6 0.0 copy-start.3
  144.6 1.2 copy-done.3
  145.9 0.0 copy-start.5
  145.9 1.5 copy.41
  147.4 9.2 %all-to-all-start.1 = ((f32[32,1,5184]{2,1,0:T(1,128)}), f32[32,1,5184]{2,1,0:T(1,128)S(1)}, u32[]{:S(2)}, u32[]{:S(2)}) async-start(f32[32,1,5184]{2,1,0:T(1,128)} %copy.41), calls=%async_computation.1 | async-start | bytes 1343488 | tf_op jit(solution)/shard_map/all_to_all | solution.py:464
  156.7 0.0 copy-done.5
  156.7 7.9 %reshape.46 = bf16[16,2,4,8,16,2,32]{6,5,4,3,2,1,0:T(2,128)(2,1)} reshape(bf16[1024,1024]{1,0:T(8,128)(2,1)S(1)} %copy-done.5) | data formatting | bytes 4194304 | tf_op jit(solution)/shard_map/reshape | solution.py:447
  164.6 1.3 dynamic-slice_reduce_fusion
  165.9 0.7 reshape.47.oo
  166.7 98.3 %ladder.1 = f32[32,5184]{1,0:T(8,128)} custom-call(bf16[2,16,32,648]{3,2,1,0:T(8,128)(2,1)} %get-tuple-element.8.tl, bf16[2,2,16,8,648]{4,3,2,1,0:T(8,128)(2,1)} %get-tuple-element.9.vl, bf16[648,5184]{1,0:T(8,128)(2,1)} %v_hbm.1, bf16[32,5184]{1,0:T(8,128)(2,1)} %copy-done.2, bf16[2,8,512]{2,1,0:T(8,128)(2,1)} %reshape.47.oo), custom_call_target="tpu_custom_call" | custom-call | tf_op jit(solution)/shard_map/ladder/pallas_call | solution.py:399
  265.0 0.0 all-to-all-done.1
  265.0 2.5 fusion.2
  (1 shorter events, 0.0 us)
Async XLA Ops:
  0.0 2.7 %copy-start.6 = (bf16[32,5184]{1,0:T(8,128)(2,1)S(1)}, bf16[32,5184]{1,0:T(8,128)(2,1)}, u32[]{:S(2)}) copy-start(bf16[32,5184]{1,0:T(8,128)(2,1)} %param.9) | copy-start | bytes 995332
  1.2 3.1 %copy-start.2 = (bf16[32,5184]{1,0:T(8,128)(2,1)}, bf16[32,5184]{1,0:T(8,128)(2,1)S(1)}, u32[]{:S(2)}) copy-start(bf16[32,5184]{1,0:T(8,128)(2,1)S(1)} %convert_element_type.7.t2) | copy-start | bytes 995332
  65.2 5.2 %copy-start.1 = (bf16[32,4,36,144]{3,0,2,1:T(8,128)(2,1)S(1)}, bf16[32,4,36,144]{3,0,2,1:T(8,128)(2,1)}, u32[]{:S(2)}) copy-start(bf16[32,4,36,144]{3,0,2,1:T(8,128)(2,1)} %copy.32) | copy-start | bytes 3981316
  90.0 15.4 %copy-start.7 = (bf16[144,4608,1]{1,0,2:T(8,128)(2,1)S(1)}, bf16[144,4608,1]{1,0,2:T(8,128)(2,1)}, u32[]{:S(2)}) copy-start(bf16[144,4608,1]{1,0,2:T(8,128)(2,1)} %reshape.51) | copy-start | bytes 3981316
  105.4 7.1 %copy-start = (bf16[4608,1152]{0,1:T(8,128)(2,1)S(1)}, bf16[4608,1152]{0,1:T(8,128)(2,1)}, u32[]{:S(2)}) copy-start(bf16[4608,1152]{0,1:T(8,128)(2,1)} %copy.35) | copy-start | bytes 31850500
  105.4 7.8 %copy-start.4 = (bf16[4608,144,1]{1,0,2:T(8,128)(2,1)S(1)}, bf16[4608,144,1]{1,0,2:T(8,128)(2,1)}, u32[]{:S(2)}) copy-start(bf16[4608,144,1]{1,0,2:T(8,128)(2,1)} %reshape.56) | copy-start | bytes 3981316
  144.6 1.2 copy-start.3
  145.9 10.8 %copy-start.5 = (bf16[1024,1024]{1,0:T(8,128)(2,1)S(1)}, bf16[1024,1024]{1,0:T(8,128)(2,1)}, u32[]{:S(2)}) copy-start(bf16[1024,1024]{1,0:T(8,128)(2,1)} %param.11) | copy-start | bytes 6291460
  147.4 117.6 %all-to-all-start.1 = ((f32[32,1,5184]{2,1,0:T(1,128)}), f32[32,1,5184]{2,1,0:T(1,128)S(1)}, u32[]{:S(2)}, u32[]{:S(2)}) async-start(f32[32,1,5184]{2,1,0:T(1,128)} %copy.41), calls=%async_computation.1 | async-start | bytes 1343488 | tf_op jit(solution)/shard_map/all_to_all | solution.py:464

commit v3 on v2

--- a/solution.py
+++ b/solution.py
@@ -25,12 +25,11 @@
     return pltpu.make_async_remote_copy(src_ref=src, dst_ref=dst, send_sem=ssem, recv_sem=rsem, device_id=dev, device_id_type=MESH)
 
 
-def gather_kernel(ts, t2, vs, tl, vl, tr, g, g_s, g_r, t_s, t_r, p_s, p_r, v_s, v_r, f_s, f_r, loc):
+def gather_kernel(ts, l1, l2, vs, wd, wx, tl, vl, w, g, lg1, lg2, wdb, wxb, wxs, d_n, e_n, w1_n, w2_n, g_s, g_r, t_s, t_r, p_s, p_r, o_s, o_r, v_s, v_r, f_s, f_r, loc, w_s):
     x, z, y, core, q = _place()
     r = lax.axis_index("row")
     right, left = (x + 1) % 4, (x + 3) % 4
     half = ts.shape[0] // 2
-    hrow = t2.shape[0] // 2
 
     own = pltpu.make_async_copy(ts, g.at[x], loc.at[0])
     own.start()
@@ -38,8 +37,19 @@
     ag_l = _rc(ts, g.at[x], g_s.at[1], g_r.at[1], (left, r))
     ag_r.start()
     ag_l.start()
-    own2 = pltpu.make_async_copy(t2, tr.at[x], loc.at[2])
+    own1 = pltpu.make_async_copy(l1, lg1.at[x], loc.at[2])
+    own2 = pltpu.make_async_copy(l2, lg2.at[x], loc.at[4])
+    own1.start()
     own2.start()
+    w_in = []
+    for i in range(4):
+        w_in.append(pltpu.make_async_copy(wd.at[pl.ds(8 * i, 8)], wdb.at[i], w_s.at[i]))
+    for i in range(4):
+        w_in.append(pltpu.make_async_copy(wx.at[:, pl.ds(32 * i + 8 * ((i + 1) // 2), 32)], wxb.at[i], w_s.at[4 + i]))
+    for i in range(2):
+        w_in.append(pltpu.make_async_copy(wx.at[:, pl.ds(32 + 72 * i, 8)], wxs.at[i], w_s.at[8 + i]))
+    for c in w_in:
+        c.start()
 
     def v_copy(x2, yd):
         return _rc(vs.at[pl.ds(2 * yd, 2), x2], vl.at[:, core, q], v_s.at[x2, yd], v_r.at[q], (x2, (x * 4 + yd) * 2 + core))
@@ -94,20 +104,74 @@
     fw_l = _rc(g.at[right, pl.ds(half, half)], g.at[right, pl.ds(half, half)], g_s.at[3], g_r.at[3], (left, r))
     fw_l.start()
     t_block(1)
-    own2.wait()
-    p_r0 = _rc(t2, tr.at[x], p_s.at[0], p_r.at[0], (right, r))
-    p_l0 = _rc(t2, tr.at[x], p_s.at[1], p_r.at[1], (left, r))
-    p_r0.start()
-    p_l0.start()
+    def ring(src, buf, ss, rr, h, ax):
+        def part(i):
+            return (pl.ds(i * h, h),) if ax == 0 else (slice(None), pl.ds(i * h, h))
+        return (_rc(src, buf.at[x], ss.at[0], rr.at[0], (right, r)), _rc(src, buf.at[x], ss.at[1], rr.at[1], (left, r)),
+                lambda: _rc(buf.at[(left,) + part(0)], buf.at[(left,) + part(0)], ss.at[2], rr.at[2], (right, r)),
+                lambda: _rc(buf.at[(right,) + part(1)], buf.at[(right,) + part(1)], ss.at[3], rr.at[3], (left, r)))
+
+    a0, a1, a2, a3 = ring(l1, lg1, p_s, p_r, l1.shape[1] // 2, 1)
+    a0.start()
+    a1.start()
+    b0, b1, b2, b3 = ring(l2, lg2, o_s, o_r, l2.shape[1] // 2, 1)
+    b0.start()
+    b1.start()
     fw_r.wait_recv()
     fw_l.wait_recv()
     t_block(2)
-    p_r0.wait_recv()
-    pf_r = _rc(tr.at[left, pl.ds(0, hrow)], tr.at[left, pl.ds(0, hrow)], p_s.at[2], p_r.at[2], (right, r))
-    pf_r.start()
-    p_l0.wait_recv()
-    pf_l = _rc(tr.at[right, pl.ds(hrow, hrow)], tr.at[right, pl.ds(hrow, hrow)], p_s.at[3], p_r.at[3], (left, r))
-    pf_l.start()
+    a0.wait_recv()
+    a2 = a2()
+    a2.start()
+    a1.wait_recv()
+    a3 = a3()
+    a3.start()
+    b0.wait_recv()
+    b2 = b2()
+    b2.start()
+    b1.wait_recv()
+    b3 = b3()
+    b3.start()
+
+    def r3_r5():
+        n1, kk = l1.shape
+        nj = wd.shape[2]
+        nb = l2.shape[0]
+        nv = wd.shape[1]
+        own1.wait()
+        own2.wait()
+        a2.wait_recv()
+        a3.wait_recv()
+        acc = None
+        for i in range(4):
+            w_in[i].wait()
+            lhs = lg1[:, :, i * 8 * nv:(i + 1) * 8 * nv].reshape(4 * n1, 8 * nv)
+            d = jnp.dot(lhs, wdb[i].reshape(8 * nv, nj), preferred_element_type=F32)
+            acc = d if acc is None else acc + d
+        for i in range(4):
+            d_n[nv // 4 * i:nv // 4 * (i + 1), :] = acc[n1 * i:n1 * i + nv // 4]
+        b2.wait_recv()
+        b3.wait_recv()
+        acc = None
+        kb = 1024
+        for i in range(4):
+            w_in[4 + i].wait()
+            d = jnp.dot(lg2[i, :, 0:kb], wxb[i].reshape(kb, nj), preferred_element_type=F32)
+            acc = d if acc is None else acc + d
+        for i in range(2):
+            w_in[8 + i].wait()
+            lhs = lg2[2 * i, :, kb:] + lg2[2 * i + 1, :, kb:]
+            acc = acc + jnp.dot(lhs, wxs[i].reshape(256, nj), preferred_element_type=F32)
+        e_n[...] = acc
+        for j in range(nj // nv):
+            w1 = d_n[:, j * nv:(j + 1) * nv] - e_n[:, j * nv:(j + 1) * nv].T
+            w1_n[:, j * nv:(j + 1) * nv] = w1
+            w2_n[:, j * nv:(j + 1) * nv] = w1.T
+        for i in range(4):
+            w[0, i, 0:nv // 4, :] = w1_n[nv // 4 * i:nv // 4 * (i + 1), :]
+            w[1, i, 0:nv // 4, :] = w2_n[nv // 4 * i:nv // 4 * (i + 1), :]
+
+    r3_r5()
 
     for k in range(16):
         qs = (q + k) % 16
@@ -130,9 +194,7 @@
         else:
             _rc(g.at[x, pl.ds(2 * y, 2)], tl.at[:, qs], t_s.at[x, y], t_r.at[qs], (x, r)).wait_recv()
     fwd.wait()
-    pf_r.wait_recv()
-    pf_l.wait_recv()
-    for c in (ag_r, ag_l, fw_r, fw_l, p_r0, p_l0, pf_r, pf_l):
+    for c in (ag_r, ag_l, fw_r, fw_l, a0, a1, a2, a3, b0, b1, b2, b3):
         c.wait_send()
     for rel in range(4):
         xs = (x + rel) % 4
@@ -147,27 +209,38 @@
     v_each(lambda a, b: v_copy(a, b).wait_send(), lambda a, b: None)
 
 
-def gather_call(ts, t2, vs):
+def gather_call(ts, l1, l2, vs, wd, wx):
     n_p, rows, cw = ts.shape
-    cols = t2.shape[1]
     dma = pltpu.SemaphoreType.DMA
     vm = pl.BlockSpec(memory_space=pltpu.VMEM)
+    hbm = pl.BlockSpec(memory_space=pl.ANY)
+    n_k, n_v, n_j = wd.shape
     return pl.pallas_call(
         gather_kernel,
         out_shape=[
             jax.ShapeDtypeStruct((2, 16, rows, cw), BF16),
             jax.ShapeDtypeStruct((2, 2, 16, rows // 4, cw), BF16),
-            jax.ShapeDtypeStruct((4, rows, cols), BF16),
+            jax.ShapeDtypeStruct((2, 4, n_v // 4 + 4, n_j), F32),
         ],
-        in_specs=[vm, vm, vm],
+        in_specs=[vm, vm, vm, vm, hbm, hbm],
         out_specs=[vm, vm, vm],
         scratch_shapes=[
             pltpu.VMEM((4, n_p, rows, cw), BF16),
-            dma((4,)), dma((4,)), dma((4, 4)), dma((16,)), dma((4,)), dma((4,)), dma((4, 4)), dma((16,)), dma, dma, dma((4,)),
+            pltpu.VMEM((4,) + l1.shape, BF16),
+            pltpu.VMEM((4,) + l2.shape, BF16),
+            pltpu.VMEM((4, 8, n_v, n_j), BF16),
+            pltpu.VMEM((4, n_k, 32, n_j), BF16),
+            pltpu.VMEM((2, n_k, 8, n_j), BF16),
+            pltpu.VMEM((n_v, n_j), F32),
+            pltpu.VMEM((n_v, n_j), F32),
+            pltpu.VMEM((n_v, n_j), F32),
+            pltpu.VMEM((n_v, n_j), F32),
+            dma((4,)), dma((4,)), dma((4, 4)), dma((16,)), dma((4,)), dma((4,)), dma((4,)), dma((4,)), dma((4, 4)), dma((16,)), dma, dma,
+            dma((5,)), dma((10,)),
         ],
         compiler_params=pltpu.CompilerParams(has_side_effects=True, vmem_limit_bytes=VMEM_LIMIT),
         name="gather",
-    )(ts, t2, vs)
+    )(ts, l1, l2, vs, wd, wx)
 
 
 N_CH = 10
@@ -175,8 +248,8 @@
 TAIL = 64
 
 
-def ladder_kernel(tl, vl, v_hbm, t2, oo, out, v_buf, t_pair, m_t, x_part, x_in, m_all, p_b, p_t, r1, r1t, r2, r2t, qb, qt,
-                  vl_s, vx_s, vx_r, tp_s, tp_r, x_s, x_r, m_s, m_r, s1, w1, s2, w2):
+def ladder_kernel(tl, vl, v_hbm, t2, oo, sw, out, s1_in, ps_in, s2_in, v_buf, t_pair, m_t, x_part, x_in, m_all, p_b, p_t, r1, r1t, r2, r2t, qb, qt,
+                  vl_s, vx_s, vx_r, tp_s, tp_r, x_s, x_r, m_s, m_r, s1, w1, s2, w2, sw_s, sw_r, ps_s, ps_r, sl):
     x, z, y, core, q = _place()
     r = lax.axis_index("row")
     mate = (x, q * 2 + 1 - core)
@@ -184,6 +257,34 @@
     n_c = v_hbm.shape[0]
     n_v = 9
     cols = [(i * 640, 640) for i in range(8)] + [(5120, 64)]
+
+    def s_copy(i, k):
+        xd = (x + k) % 4
+        return _rc(sw.at[i, xd], (s1_in, s2_in)[i].at[x], sw_s.at[i, k], sw_r.at[i, k], (xd, r))
+
+    s_own = [pltpu.make_async_copy(sw.at[i, x], (s1_in, s2_in)[i].at[x], sl.at[i]) for i in range(2)]
+    for i in (1, 0):
+        for k in range(1, 4):
+            s_copy(i, k).start()
+        s_own[i].start()
+
+    def ps_src(rd):
+        j = rd % 8
+        return s2_in.at[rd // 8, :, pl.ds(pl.multiple_of(9 * j // 8 * 128, 128), 256)]
+
+    def ps_copy(k):
+        rd = (r + k) % 32
+        return _rc(ps_src(rd), ps_in.at[r], ps_s.at[k], ps_r.at[k], (x, rd))
+
+    ps_own = pltpu.make_async_copy(ps_src(r), ps_in.at[r], sl.at[2])
+
+    def ps_send():
+        s_own[1].wait()
+        for k in range(1, 4):
+            s_copy(1, k).wait_recv()
+        ps_own.start()
+        for k in range(1, 32):
+            ps_copy(k).start()
 
     v_in = []
     v_x = []
@@ -355,6 +456,7 @@
         l1(t, kind(t), pb, rb, col0(t), CW)
         return c
     lax.fori_loop(0, N_CH, f1, 0)
+    ps_send()
     l2(N_CH, 1, p_t, r1t)
 
     def f2(t, c):
@@ -387,9 +489,16 @@
         x_copy(k).wait_send()
     for k in range(1, 4):
         m_copy(k).wait_send()
-
-
-def ladder_call(tl, vl, v, t2, oo):
+    s_own[0].wait()
+    ps_own.wait()
+    for k in range(1, 32):
+        ps_copy(k).wait()
+    for k in range(1, 4):
+        s_copy(0, k).wait()
+        s_copy(1, k).wait_send()
+
+
+def ladder_call(tl, vl, v, t2, oo, sw):
     _, _, rows, n_c = tl.shape
     k8 = vl.shape[3]
     cols = t2.shape[1]
@@ -398,10 +507,15 @@
     n = N_CH + 1
     return pl.pallas_call(
         ladder_kernel,
-        out_shape=jax.ShapeDtypeStruct((rows, cols), F32),
-        in_specs=[vm, vm, pl.BlockSpec(memory_space=pl.ANY), vm, vm],
-        out_specs=vm,
+        out_shape=[
+            jax.ShapeDtypeStruct((rows, cols), F32),
+            jax.ShapeDtypeStruct(sw.shape[1:], F32),
+            jax.ShapeDtypeStruct((32, sw.shape[2], 256), F32),
+        ],
+        in_specs=[vm, vm, pl.BlockSpec(memory_space=pl.ANY), vm, vm, vm],
+        out_specs=[vm, vm, vm],
         scratch_shapes=[
+            pltpu.VMEM(sw.shape[1:], F32),
             pltpu.VMEM((2, n_c, cols), BF16),
             pltpu.VMEM((2, rows, cols), BF16),
             pltpu.VMEM((16 * rows, 8 * k8), BF16),
@@ -417,11 +531,11 @@
             pltpu.VMEM((8, 128), F32),
             pltpu.VMEM((8, 128), F32),
             dma((9,)), dma((9,)), dma((9,)), dma((2,)), dma, dma((16,)), dma((16,)), dma((4,)), dma((4,)),
-            dma((n, 6)), dma((n, 6)), dma((n, 6)), dma((n, 6)),
+            dma((n, 6)), dma((n, 6)), dma((n, 6)), dma((n, 6)), dma((2, 4)), dma((2, 4)), dma((32,)), dma((32,)), dma((3,)),
         ],
         compiler_params=pltpu.CompilerParams(has_side_effects=True, vmem_limit_bytes=VMEM_LIMIT),
         name="ladder",
-    )(tl, vl, v, t2, oo)
+    )(tl, vl, v, t2, oo, sw)
 
 
 def solution(mesh):
@@ -443,26 +557,26 @@
         t_half = t_blk.astype(BF16)
         ts = t_half.reshape(rows_dev, n_p, c_dev).transpose(1, 0, 2)
         vs = oovv_blk.reshape(n_col, occ_col, n_p, c_dev).transpose(2, 0, 1, 3)
-        tl, vl, tr = gather_call(ts, t_half, vs)
-        oo = oooo_full.reshape(16, 2, n_col, occ_col, 16, 2, n_occ)
-        oo = lax.dynamic_index_in_dim(oo, q, 0, False)
-        oo = lax.dynamic_index_in_dim(oo, lax.axis_index("col"), 1, False)
-        oo = lax.dynamic_index_in_dim(oo, core, 3, False)
-        oo = oo.reshape(2, occ_col, 16 * n_occ)
-        ladder_sum = ladder_call(tl, vl, vvvv_blk, t_half, oo)
-
-        t_four = tr.reshape(n_col, n_occ, virt_col, n_virt).transpose(1, 0, 2, 3).reshape(n_occ, n_virt, n_virt)
-        lhs_d = t_four.transpose(1, 0, 2).reshape(n_virt, n_occ * n_virt)
-        lhs_x = t_four.reshape(n_occ * n_virt, n_virt)
-        out_d = jnp.dot(lhs_d, wd_blk, preferred_element_type=F32).reshape(n_virt, occ_col, n_virt)
-        out_x = lax.dot_general(lhs_x, wx_blk, (((0,), (0,)), ((), ())), preferred_element_type=F32).reshape(n_virt, occ_col, n_virt)
-        s_ab = out_d - out_x.transpose(2, 1, 0)
-        s_ba = s_ab.transpose(2, 1, 0)
-        pair = jnp.stack([s_ab.transpose(1, 0, 2), s_ba.transpose(1, 0, 2)])
-        pair = pair.reshape(2, occ_col, n_col, virt_col * n_virt)
-        pair = lax.all_to_all(pair, "col", 2, 1, tiled=True).reshape(2, n_occ, cols_dev)
-        swapped = lax.all_to_all(pair[1], "row", 0, 0, tiled=True)
-        ph_sym = pair[0] + swapped
+        t3 = t_half.reshape(n_occ, virt_col, n_virt)
+        l1 = t3.transpose(1, 0, 2).reshape(virt_col, n_occ * n_virt)
+        l1 = jnp.pad(l1, ((0, 12), (0, 0)))
+        tb = t3.transpose(2, 0, 1)
+        odd = lax.axis_index("col") % 2 == 1
+        z4 = jnp.zeros((n_virt, n_occ, 4), BF16)
+        full = jnp.where(odd, tb[:, :, 4:], tb[:, :, :32]).reshape(n_virt, n_occ * 32)
+        edge = jnp.where(odd, jnp.concatenate([z4, tb[:, :, :4]], axis=2), jnp.concatenate([tb[:, :, 32:], z4], axis=2))
+        l2 = jnp.concatenate([full, edge.reshape(n_virt, n_occ * 8)], axis=1)
+        wd3 = wd_blk.reshape(n_occ, n_virt, occ_col * n_virt)
+        wx3 = wx_blk.reshape(n_occ, n_virt, occ_col * n_virt)
+        tl, vl, sw = gather_call(ts, l1, l2, vs, wd3, wx3)
+        start = q * 2 * n_occ + lax.axis_index("col") * occ_col
+        oo = jnp.stack([lax.dynamic_slice_in_dim(oooo_full, start + i * n_occ, occ_col, axis=0) for i in range(2)])
+        oo = oo.reshape(2, occ_col, 16, 2, n_occ)
+        oo = jnp.where(core == 1, oo[:, :, :, 1], oo[:, :, :, 0]).reshape(2, occ_col, 16 * n_occ)
+        ladder_sum, s1, ps = ladder_call(tl, vl, vvvv_blk, t_half, oo, sw)
+        s1 = s1[:, :virt_col].reshape(n_col, virt_col, occ_col, n_virt).transpose(0, 2, 1, 3).reshape(n_occ, cols_dev)
+        ps = lax.dynamic_slice_in_dim(ps[:, :virt_col], 16 * (lax.axis_index("row") % 8), n_virt, axis=2).reshape(n_occ, cols_dev)
+        ph_sym = s1 + ps
         residual = oovv_blk.astype(F32) + ladder_sum + ph_sym
         return residual / d_blk
 

time: 269 us -> 208 us (0.77)
  local copies, waits for them, and re-layouts: 70.5 us -> 13.2 us
  Pallas kernels: 151 us -> 191 us
  blocking collectives: 21.4 us -> 0 us
  matrix products: 10.2 us -> 0 us
  starting transfers between devices: 9.22 us -> 0 us
    unnamed x18 -> x7, local copies, waits for them, and re-layouts: 33.9 us -> 0.06 us
    pallas_call x1, Pallas kernels: 98.3 us -> 121 us  [ladder_call(): pl.pallas_call(ladder_kernel, out_shape=[jax.ShapeDtypeStruct((rows, cols...]
    all_to_all x1 -> x0, blocking collectives: 21.4 us -> none  [local_sweep(): lax.all_to_all(pair, 'col', 2, 1, tiled=True).reshape(2, n_occ, cols_dev)]
    pallas_call x1, Pallas kernels: 52.4 us -> 69.9 us  [gather_call(): pl.pallas_call(gather_kernel, out_shape=[jax.ShapeDtypeStruct((2, 16, row...]
    reshape x4 -> x7, local copies, waits for them, and re-layouts: 17.5 us -> 3.65 us  [the longest x2 1.3 us: local_sweep(): s1[:, :virt_col].reshape(n_col, virt_col, occ_col, n_virt)]
    dot_general x2 -> x0, matrix products: 10.2 us -> none  [the longest x1 5.79 us: local_sweep(): jnp.dot(lhs_d, wd_blk, preferred_element_type=F32)]
    all_to_all x1 -> x0, starting transfers between devices: 9.22 us -> none  [local_sweep(): swapped = lax.all_to_all(pair[1], 'row', 0, 0, tiled=True)]
    another operation x4 -> x3, local copies, waits for them, and re-layouts: 7.43 us -> 0.28 us  [local_sweep(): jnp.stack([lax.dynamic_slice_in_dim(oooo_full, start + i * n_occ, occ_col...]
  transfers between devices with their start and end apart: 1 -> 0, of which waited for: 0 -> 0; matrix products, arithmetic and copies ran while one was open for 4% -> 0% of each run, Pallas kernels for 37% -> 0%
where the time goes in v3:
time: 208 us
  Pallas kernels  191 us (92%)
  local copies, waits for them, and re-layouts  13.2 us (6%)
  other arithmetic  3.83 us (2%)
    pallas_call x1, Pallas kernels, ladder_call(): pl.pallas_call(ladder_kernel, out_shape=[jax.ShapeDtypeStruct((rows, cols...  121 us
    pallas_call x1, Pallas kernels, gather_call(): pl.pallas_call(gather_kernel, out_shape=[jax.ShapeDtypeStruct((2, 16, row...  69.9 us

profile of v3, /device:TPU:0, one launch (start us, length us, event | category | flops | bytes accessed | tf_op | source)
XLA Modules:
  0.0 208.2 jit_solution(13634284256280618722)
XLA Ops:
  0.0 0.0 copy-start.2
  0.0 0.8 constant_dynamic-slice_fusion.1
  0.8 0.1 stack.10
  0.9 0.1 stack.9
  1.1 0.1 constant_dynamic-update-slice_fusion
  1.2 0.0 copy-start.1
  1.2 0.5 fusion
  1.7 0.7 select_n.67.oo
  2.4 0.0 copy-done.2
  2.4 0.0 copy-start
  2.4 0.7 reshape.43
  3.1 0.8 copy.30
  3.9 0.0 copy-done.1
  3.9 0.7 reshape.48
  4.7 0.8 copy.29
  5.5 0.0 copy-done
  5.5 0.8 reshape.44
  6.3 0.1 select_bitcast_fusion
  6.4 0.1 copy.23
  6.5 0.1 slice_select_fusion
  6.7 0.2 copy.22
  6.8 0.8 pad_maximum_fusion.l2
  7.6 0.1 copy.21
  7.8 0.8 reshape.45
  8.6 0.8 pad.6.l1
  9.4 69.9 %gather.1 = (bf16[2,16,32,648]{3,2,1,0:T(8,128)(2,1)}, bf16[2,2,16,8,648]{4,3,2,1,0:T(8,128)(2,1)}, f32[2,4,40,1152]{3,2,1,0:T(8,128)}) custom-call(bf16[8,32,648]{2,1,0:T(8,128)(2,1)} %bitcast.27, bf16[48,4608]{1,0:T(8,128)(2,1)} %pad.6.l1, bf16[144,1280]{1,0:T(8,128)(2,1)} %pad_maximum_fusion.l2, bf16[8,4,8,648]{3,2,1,0:T(8,128)(2,1)} %bitcast.28, ...), custom_call_target="tpu_custom_call" | custom-call | tf_op jit(solution)/shard_map/gather/pallas_call | solution.py:218
  79.2 121.1 %ladder.1 = (f32[32,5184]{1,0:T(8,128)}, f32[4,40,1152]{2,1,0:T(8,128)}, f32[32,40,256]{2,1,0:T(8,128)}) custom-call(bf16[2,16,32,648]{3,2,1,0:T(8,128)(2,1)} %get-tuple-element.11.tl, bf16[2,2,16,8,648]{4,3,2,1,0:T(8,128)(2,1)} %get-tuple-element.12.vl, bf16[648,5184]{1,0:T(8,128)(2,1)} %v_hbm.1, bf16[32,5184]{1,0:T(8,128)(2,1)} %copy-done, ...), custom_call_target="tpu_custom_call" | custom-call | tf_op jit(solution)/shard_map/ladder/pallas_call | solution.py:508
  200.4 1.3 copy.25
  201.7 0.8 reshape.51
  202.5 0.7 copy.26
  203.2 0.5 reshape.52
  203.7 1.7 constant_dynamic-slice_fusion
  205.4 0.5 reshape.53
  205.9 2.3 %add_divide_fusion = f32[32,5184]{1,0:T(8,128)} fusion(f32[32,5184]{1,0:T(8,128)} %param.8, f32[32,5184]{1,0:T(8,128)S(1)} %reshape.52, f32[32,5184]{1,0:T(8,128)S(1)} %reshape.53, f32[32,5184]{1,0:T(8,128)} %get-tuple-element.14, bf16[32,5184]{1,0:T(8,128)(2,1)S(1)} %copy-done.1), kind=kLoop, calls=%fused_computation | loop fusion | flops 829440 | bytes 3649536 | tf_op jit(solution)/shard_map/div | solution.py:581
  (3 shorter events, 0.1 us)
Async XLA Ops:
  0.0 2.4 %copy-start.2 = (f32[32,5184]{1,0:T(8,128)S(1)}, f32[32,5184]{1,0:T(8,128)}, u32[]{:S(2)}) copy-start(f32[32,5184]{1,0:T(8,128)} %param.7) | copy-start | bytes 1990660
  1.2 2.8 %copy-start.1 = (bf16[32,5184]{1,0:T(8,128)(2,1)S(1)}, bf16[32,5184]{1,0:T(8,128)(2,1)}, u32[]{:S(2)}) copy-start(bf16[32,5184]{1,0:T(8,128)(2,1)} %param.9) | copy-start | bytes 995332
  2.4 3.1 %copy-start = (bf16[32,5184]{1,0:T(8,128)(2,1)}, bf16[32,5184]{1,0:T(8,128)(2,1)S(1)}, u32[]{:S(2)}) copy-start(bf16[32,5184]{1,0:T(8,128)(2,1)S(1)} %convert_element_type.9.t2) | copy-start | bytes 995332

commit v4 on v0

v4 whole, which is shorter than its diff:
```python
import math
import jax
import jax.numpy as jnp
from jax import lax
from jax.experimental import pallas as pl
from jax.experimental.pallas import tpu as pltpu
from jax.sharding import PartitionSpec as P

MESH = pl.DeviceIdType.MESH
BF16 = jnp.bfloat16
F32 = jnp.float32
VMEM_LIMIT = 67_043_328
LANE = 128
RING = 4
PLANE = 16
ROWS = 32
FULL = 32
EDGE = 8
N_CH = 10
CW = 512
TAIL = 64


def _place():
    x = lax.axis_index("col")
    r = lax.axis_index("row")
    q = r // 2
    return x, q // RING, q % RING, r % 2, q, r


def _rc(src, dst, ssem, rsem, dev):
    return pltpu.make_async_remote_copy(src_ref=src, dst_ref=dst, send_sem=ssem, recv_sem=rsem, device_id=dev, device_id_type=MESH)


def _enter(x, z, core, r):
    bar = pltpu.get_barrier_semaphore()

    def tell(dev):
        pl.semaphore_signal(bar, inc=1, device_id=dev, device_id_type=MESH)

    for k in range(1, RING):
        tell(((x + k) % RING, r))
    for k in range(1, ROWS):
        tell((x, (r + k) % ROWS))

    @pl.when(x != z)
    def _():
        for k in range(PLANE):
            tell((z, k * 2 + core))

    pl.semaphore_wait(bar, RING - 1 + ROWS - 1 + RING * (RING - 1))


def sweep_kernel(ts, l1, l2, vs, wd, wx, v_hbm, t2, oo, out, s1_in, ps_in,
                 g, tl, vl, lg1, lg2, wdb, wxb, wxs, d_n, e_n, sw, s2_in, v_buf, t_pair, m_t, x_part, x_in, m_all,
                 p_b, p_t, r1, r1t, r2, r2t,
                 g_s, g_r, t_s, t_r, p_s, p_r, o_s, o_r, v_s, v_r, f_s, f_r, loc, wd_s, wx_s, wy_s,
                 vl_s, vx_s, vx_r, tp_s, tp_r, x_s, x_r, m_s, m_r, s1, w1, s2, w2, sw_s, sw_r, ps_s, ps_r):
    x, z, y, core, q, r = _place()
    right, left = (x + 1) % RING, (x + RING - 1) % RING
    mate = (x, q * 2 + 1 - core)
    n_kd, n_v, n_j = wd.shape
    rows, n_c = tl.shape[2:]
    loc_g, loc_t, loc_1, loc_2, loc_v, loc_p, loc_a, loc_b = [loc.at[i] for i in range(loc.shape[0])]
    _enter(x, z, core, r)

    def ring(src, buf, ss, rr, axis):
        h = src.shape[axis] // 2

        def part(i):
            return (pl.ds(i * h, h),) if axis == 0 else (slice(None), pl.ds(i * h, h))

        def hop(i, who, blk, to):
            ref = buf.at[(blk,) + part(i - 2)]
            return _rc(ref, ref, ss.at[i], rr.at[i], (to, who))

        c0 = _rc(src, buf.at[x], ss.at[0], rr.at[0], (right, r))
        c1 = _rc(src, buf.at[x], ss.at[1], rr.at[1], (left, r))
        return c0, c1, lambda: hop(2, r, left, right), lambda: hop(3, r, right, left)

    own = pltpu.make_async_copy(ts, g.at[x], loc_g)
    own1 = pltpu.make_async_copy(l1, lg1.at[x], loc_1)
    own2 = pltpu.make_async_copy(l2, lg2.at[x], loc_2)
    g0, g1, g2, g3 = ring(ts, g, g_s, g_r, 0)
    own.start()
    g0.start()
    g1.start()
    own1.start()
    own2.start()

    def wd_copy(i):
        return pltpu.make_async_copy(wd.at[pl.ds(EDGE * i, EDGE)], wdb.at[i % 2], wd_s.at[i % 2])

    def wx_copy(i):
        c, h = i // 2, n_kd // 2
        src = wx.at[pl.ds(i % 2 * h, h), pl.ds(FULL * c + EDGE * ((c + 1) // 2), FULL)]
        return pltpu.make_async_copy(src, wxb.at[i % 2], wx_s.at[i % 2])

    def wy_copy(i):
        return pltpu.make_async_copy(wx.at[:, pl.ds(FULL + n_v // 2 * i, EDGE)], wxs.at[i], wy_s.at[i])

    for i in range(2):
        wd_copy(i).start()
        wx_copy(i).start()
        wy_copy(i).start()

    def v_copy(x2, yd):
        return _rc(vs.at[pl.ds(2 * yd, 2), x2], vl.at[:, core, q], v_s.at[x2, yd], v_r.at[q], (x2, (x * RING + yd) * 2 + core))

    def v_arrival(k):
        return _rc(vs.at[pl.ds(2 * y, 2), x], vl.at[:, core, (q + k) % PLANE], v_s.at[x, y], v_r.at[(q + k) % PLANE], (x, r))

    v_own = pltpu.make_async_copy(vs.at[pl.ds(2 * y, 2), x], vl.at[:, core, q], loc_v)

    def v_each(act, act_own):
        for i in range(RING):
            for k in range(RING):
                c = v_copy((x + i) % RING, (y + k) % RING)
                if i + k == 0:
                    if act_own is not None:
                        pl.when(x == z)(act_own)
                    pl.when(x != z)(lambda: act(c))
                else:
                    act(c)

    def t_copy(xs, yd):
        return _rc(g.at[xs, pl.ds(2 * yd, 2)], tl.at[:, q], t_s.at[xs, yd], t_r.at[q], (x, (xs * RING + yd) * 2 + core))

    def t_arrival(k):
        return _rc(g.at[x, pl.ds(2 * y, 2)], tl.at[:, (q + k) % PLANE], t_s.at[x, y], t_r.at[(q + k) % PLANE], (x, r))

    def t_block(rel):
        xs = (x + rel) % RING
        for k in range(RING):
            yd = (y + k) % RING
            if k == 0:
                pl.when(xs == z)(lambda: pltpu.make_async_copy(g.at[xs, pl.ds(2 * yd, 2)], tl.at[:, q], loc_t).start())
                pl.when(xs != z)(lambda: t_copy(xs, yd).start())
            else:
                t_copy(xs, yd).start()

    own.wait()
    t_block(0)
    v_each(lambda c: c.start(), v_own.start)
    g0.wait_recv()
    g2 = g2()
    g2.start()
    t_block(RING - 1)
    g1.wait_recv()
    g3 = g3()
    g3.start()
    t_block(1)
    a0, a1, a2, a3 = ring(l1, lg1, p_s, p_r, 1)
    b0, b1, b2, b3 = ring(l2, lg2, o_s, o_r, 1)
    for c in (a0, a1, b0, b1):
        c.start()
    g2.wait_recv()
    g3.wait_recv()
    t_block(2)

    n_v9 = vl_s.shape[0]
    wide = 640
    v_in = []
    for i in range(n_v9):
        c0 = i * wide
        w = min(wide, v_hbm.shape[1] - c0)
        src, dst = v_hbm.at[:, pl.ds(c0, w)], v_buf.at[core, :, pl.ds(c0, w)]
        v_in += [pltpu.make_async_copy(src, dst, vl_s.at[i]), _rc(src, dst, vx_s.at[i], vx_r.at[i], mate)]
    v_in += [pltpu.make_async_copy(t2, t_pair.at[core], loc_p), _rc(t2, t_pair.at[core], tp_s, tp_r, mate)]
    for c in v_in:
        c.start()

    pl.when(x == z)(v_own.wait)
    pl.when(x != z)(lambda: v_arrival(0).wait_recv())
    for k in range(1, PLANE):
        v_arrival(k).wait_recv()
    fwd = _rc(vl.at[:, core], vl.at[:, core], f_s, f_r, mate)
    fwd.start()
    a0.wait_recv()
    a2 = a2()
    a2.start()
    a1.wait_recv()
    a3 = a3()
    a3.start()
    pltpu.make_async_copy(g.at[x, pl.ds(2 * y, 2)], tl.at[:, q], loc_t).wait()
    for k in range(1, PLANE):
        t_arrival(k).wait_recv()
    fwd.wait()

    k8 = vl.shape[3]
    n_i = PLANE * rows
    n_k = 2 * PLANE * k8
    dn = (((1,), (1,)), ((), ()))
    xp = [lax.dot_general(vl[i].reshape(n_k, n_c), tl[i].reshape(n_i, n_c), dn, preferred_element_type=F32) for i in range(2)]
    x_part[...] = (xp[0] + xp[1]).reshape(2, PLANE, k8, n_i)

    def x_copy(k):
        qd = (q + k) % PLANE
        return _rc(x_part.at[:, qd], x_in.at[q], x_s.at[k], x_r.at[k], (x, qd * 2 + core))

    for k in range(1, PLANE):
        x_copy(k).start()
    x_in[q] = x_part[:, q]
    b0.wait_recv()
    b2 = b2()
    b2.start()
    b1.wait_recv()
    b3 = b3()
    b3.start()

    n1 = l1.shape[0]
    quarter = n_v // RING
    own1.wait()
    own2.wait()
    a2.wait_recv()
    a3.wait_recv()
    acc = None
    for i in range(RING):
        wd_copy(i).wait()
        lhs = lg1[:, :, i * EDGE * n_v:(i + 1) * EDGE * n_v].reshape(RING * n1, EDGE * n_v)
        d = jnp.dot(lhs, wdb[i % 2].reshape(EDGE * n_v, n_j), preferred_element_type=F32)
        acc = d if acc is None else acc + d
        if i < 2:
            wd_copy(i + 2).start()
    for i in range(RING):
        d_n[quarter * i:quarter * (i + 1), :] = acc[n1 * i:n1 * i + quarter]
    b2.wait_recv()
    b3.wait_recv()
    acc = None
    kb = FULL * n_kd
    kh = kb // 2
    for i in range(2 * RING):
        wx_copy(i).wait()
        d = jnp.dot(lg2[i // 2, :, i % 2 * kh:(i % 2 + 1) * kh], wxb[i % 2].reshape(kh, n_j), preferred_element_type=F32)
        acc = d if acc is None else acc + d
        if i + 2 < 2 * RING:
            wx_copy(i + 2).start()
    for i in range(2):
        wy_copy(i).wait()
        lhs = lg2[2 * i, :, kb:] + lg2[2 * i + 1, :, kb:]
        acc = acc + jnp.dot(lhs, wxs[i].reshape(EDGE * n_kd, n_j), preferred_element_type=F32)
    e_n[...] = acc

    for k in range(1, PLANE):
        x_copy(k).wait_recv()
    xs = x_in[0]
    for k in range(1, PLANE):
        xs = xs + x_in[k]
    m_all[x] = (oo[...].astype(F32) + 0.5 * xs).astype(BF16)

    def m_copy(k):
        return _rc(m_all.at[x], m_all.at[x], m_s.at[k], m_r.at[k], ((x + k) % RING, r))

    for k in range(1, RING):
        m_copy(k).start()

    for j in range(n_j // n_v):
        cut = slice(j * n_v, (j + 1) * n_v)
        sj = d_n[:, cut] - e_n[:, cut].T
        d_n[:, cut] = sj
        e_n[:, cut] = sj.T
    for i in range(RING):
        sw[0, i, :quarter, :] = d_n[quarter * i:quarter * (i + 1), :]
        sw[1, i, :quarter, :] = e_n[quarter * i:quarter * (i + 1), :]

    def s_copy(i, k):
        xd = (x + k) % RING
        return _rc(sw.at[i, xd], (s1_in, s2_in)[i].at[x], sw_s.at[i, k], sw_r.at[i, k], (xd, r))

    s_own = [pltpu.make_async_copy(sw.at[i, x], (s1_in, s2_in)[i].at[x], (loc_a, loc_b)[i]) for i in range(2)]
    for i in (1, 0):
        for k in range(1, RING):
            s_copy(i, k).start()
        s_own[i].start()

    def ps_src(rd):
        return s2_in.at[rd // EDGE, :, pl.ds(pl.multiple_of(rd % EDGE * 9 // EDGE * LANE, LANE), 2 * LANE)]

    def ps_copy(k):
        rd = (r + k) % ROWS
        return _rc(ps_src(rd), ps_in.at[r], ps_s.at[k], ps_r.at[k], (x, rd))

    ps_own = pltpu.make_async_copy(ps_src(r), ps_in.at[r], loc_g)

    def ps_send():
        s_own[1].wait()
        for k in range(1, RING):
            s_copy(1, k).wait_recv()
        ps_own.start()
        for k in range(1, ROWS):
            ps_copy(k).start()

    for c in v_in:
        c.wait()
    for k in range(1, RING):
        m_copy(k).wait_recv()
    mf = m_all[...].astype(F32)
    m_t[...] = jnp.concatenate([mf[xx, cc] for cc in range(2) for xx in range(RING)], axis=0).T.astype(BF16)

    def to(first, a, d):
        b = a if first else 1 - a
        return (x, (((z + d * (1 - b)) % RING) * RING + (y + d * b) % RING) * 2 + core)

    def coords(a):
        return y * a + z * (1 - a), z * a + y * (1 - a)

    def stage(first, t, a, pb, rb):
        u, v = coords(a)
        c, pre, n = (u, (), 2) if first else (v, (u,), rows // 2)
        lo, hi = pl.ds(0, n), pl.ds(n, n)
        far, up, dn_ = (c + 2) % RING, (c + 1) % RING, (c + RING - 1) % RING
        ss, ww = (s1, w1) if first else (s2, w2)
        srcs = (far, lo), (far, hi), (up, hi), (dn_, lo), (up, lo), (dn_, hi)

        def msg(i):
            d = 1 if i % 2 == 0 else RING - 1
            return _rc(pb.at[pre + srcs[i]], rb.at[i], ss.at[t, i], ww.at[t, i], to(first, a, d))
        return msg

    near = range(2, 6)

    def l1_step(t, a, pb, rb, c0, w):
        tp = t_pair[:, :, pl.ds(c0, w)].reshape(2 * rows, w)
        acc = jnp.dot(m_t[...], tp, preferred_element_type=F32)
        for i in range(2):
            acc = acc + jnp.dot(tl[i].reshape(n_i, n_c), v_buf[i, :, pl.ds(c0, w)], preferred_element_type=F32)
        for zb in range(RING):
            for yb in range(RING):
                b = (zb * RING + yb) * rows
                pb[yb * a + zb * (1 - a), zb * a + yb * (1 - a)] = acc[b:b + rows]
        msg = stage(True, t, a, pb, rb)
        for i in range(4):
            msg(i).start()

    def add_step(first, t, a, pb, rb):
        u, v = coords(a)
        c, pre, n = (u, (), 2) if first else (v, (u,), rows // 2)
        msg = stage(first, t, a, pb, rb)
        msg(0).wait_recv()
        up = pre + ((c + 1) % RING, pl.ds(0, n))
        pb[up] = pb[up] + rb[0]
        msg(4).start()
        msg(1).wait_recv()
        dn_ = pre + ((c + RING - 1) % RING, pl.ds(n, n))
        pb[dn_] = pb[dn_] + rb[1]
        msg(5).start()

    def l3_step(t, a, pb, rb, rb2):
        u, _ = coords(a)
        msg = stage(True, t, a, pb, rb)
        for i in near:
            msg(i).wait_recv()
        pb[u, :2] = pb[u, :2] + rb[4] + rb[3]
        pb[u, 2:] = pb[u, 2:] + rb[2] + rb[5]
        nxt = stage(False, t, a, pb, rb2)
        for i in range(4):
            nxt(i).start()

    def l5_step(t, a, pb, rb, rb2, c0, w):
        u, v = coords(a)
        h = rows // 2
        msg, old = stage(False, t, a, pb, rb2), stage(True, t, a, pb, rb)
        for i in near:
            msg(i).wait_recv()
        out[:h, pl.ds(c0, w)] = pb[u, v, :h] + rb2[4] + rb2[3]
        out[h:, pl.ds(c0, w)] = pb[u, v, h:] + rb2[2] + rb2[5]
        for i in range(6):
            msg(i).wait_send()
            old(i).wait_send()

    def at(t):
        return (t, 1 - t % 2, p_b.at[t], r1.at[t], r2.at[t])

    def col0(t):
        return pl.multiple_of((t // 2) * CW + (t % 2) * (N_CH // 2) * CW, LANE)

    def loop(lo, fn):
        lax.fori_loop(lo, N_CH, lambda t, c: (fn(t), c)[1], 0)

    tail = (N_CH, 1, p_t, r1t, r2t)
    ct = N_CH * CW

    def run1(t):
        n, a, pb, rb, _ = at(t)
        l1_step(n, a, pb, rb, col0(t), CW)

    def run3(t):
        l3_step(*at(t))
        n, a, pb, _, rb2 = at(t - 1)
        add_step(False, n, a, pb, rb2)

    l1_step(*tail[:4], ct, TAIL)
    loop(0, run1)
    ps_send()
    add_step(True, *tail[:4])
    loop(0, lambda t: add_step(True, *at(t)[:4]))
    l3_step(*tail)
    add_step(False, *tail[:3], r2t)
    l3_step(*at(0))
    loop(1, run3)
    n, a, pb, _, rb2 = at(N_CH - 1)
    add_step(False, n, a, pb, rb2)
    l5_step(*tail, ct, TAIL)
    loop(0, lambda t: l5_step(*at(t), col0(t), CW))

    for c in (g0, g1, g2, g3, a0, a1, a2, a3, b0, b1, b2, b3):
        c.wait_send()
    for rel in range(RING):
        xs = (x + rel) % RING
        for k in range(RING):
            c = t_copy(xs, (y + k) % RING)
            if k == 0:
                pl.when(xs != z)(c.wait_send)
            else:
                c.wait_send()
    v_each(lambda c: c.wait_send(), None)
    for k in range(1, PLANE):
        x_copy(k).wait_send()
    for k in range(1, RING):
        m_copy(k).wait_send()
        s_copy(0, k).wait()
        s_copy(1, k).wait_send()
    s_own[0].wait()
    ps_own.wait()
    for k in range(1, ROWS):
        ps_copy(k).wait()


def sweep_call(ts, l1, l2, vs, wd, wx, v, t2, oo):
    n_p, rows, n_c = ts.shape
    n_k, n_v, n_j = wd.shape
    cols = t2.shape[1]
    k8 = rows // RING
    n_i = PLANE * rows
    blk = (n_v // RING + RING, n_j)
    n = N_CH + 1
    dma = pltpu.SemaphoreType.DMA
    vm = pl.BlockSpec(memory_space=pltpu.VMEM)
    hbm = pl.BlockSpec(memory_space=pl.ANY)

    def b16(*shape):
        return pltpu.VMEM(shape, BF16)

    def f32(*shape):
        return pltpu.VMEM(shape, F32)

    def sems(*shape):
        return dma(shape)

    one, two, four, six = (), (2,), (RING,), (n, 6)
    all16, sq = (PLANE,), (RING, RING)
    v9 = (-(-cols // 640),)
    counts = [four, four, sq, all16, four, four, four, four, sq, all16, one, one, (8,), two, two, two,
              v9, v9, v9, one, one, all16, all16, four, four, six, six, six, six, (2, RING), (2, RING), (ROWS,), (ROWS,)]
    return pl.pallas_call(
        sweep_kernel,
        out_shape=[
            jax.ShapeDtypeStruct((rows, cols), F32),
            jax.ShapeDtypeStruct((RING,) + blk, F32),
            jax.ShapeDtypeStruct((ROWS, blk[0], 2 * LANE), F32),
        ],
        in_specs=[vm, vm, vm, vm, hbm, hbm, hbm, vm, vm],
        out_specs=[vm, vm, vm],
        scratch_shapes=[
            b16(RING, n_p, rows, n_c), b16(2, PLANE, rows, n_c), b16(2, 2, PLANE, k8, n_c),
            b16(RING, *l1.shape), b16(RING, *l2.shape),
            b16(2, EDGE, n_v, n_j), b16(2, n_k // 2, FULL, n_j), b16(2, n_k, EDGE, n_j),
            f32(n_v, n_j), f32(n_v, n_j), f32(2, RING, *blk), f32(RING, *blk),
            b16(2, n_c, cols), b16(2, rows, cols), b16(n_i, 2 * rows),
            f32(2, PLANE, k8, n_i), f32(PLANE, 2, k8, n_i), b16(RING, 2, k8, n_i),
            f32(N_CH, RING, RING, rows, CW), f32(RING, RING, rows, TAIL),
            f32(N_CH, 6, 2, rows, CW), f32(6, 2, rows, TAIL),
            f32(N_CH, 6, rows // 2, CW), f32(6, rows // 2, TAIL),
        ] + [sems(*c) if c else dma for c in counts],
        compiler_params=pltpu.CompilerParams(has_side_effects=True, collective_id=0, vmem_limit_bytes=VMEM_LIMIT),
        name="sweep",
    )(ts, l1, l2, vs, wd, wx, v, t2, oo)


def solution(mesh):
    n_col = mesh.shape["col"]
    amp_spec = P("row", "col")
    wide_spec = P(None, "col")

    def local_sweep(t_blk, d_blk, oovv_blk, vvvv_blk, oooo_full, wd_blk, wx_blk):
        rows_dev, cols_dev = t_blk.shape
        n_occ = math.isqrt(oooo_full.shape[0])
        n_virt = wd_blk.shape[0] // n_occ
        occ_col = n_occ // n_col
        virt_col = n_virt // n_col
        c_dev = vvvv_blk.shape[0]
        n_p = cols_dev // c_dev
        x = lax.axis_index("col")
        r = lax.axis_index("row")
        t_half = t_blk.astype(BF16)
        ts = t_half.reshape(rows_dev, n_p, c_dev).transpose(1, 0, 2)
        vs = oovv_blk.reshape(n_col, occ_col, n_p, c_dev).transpose(2, 0, 1, 3)
        t3 = t_half.reshape(n_occ, virt_col, n_virt)
        l1 = t3.transpose(1, 0, 2).reshape(virt_col, n_occ * n_virt)
        l1 = jnp.pad(l1, ((0, 12), (0, 0)))
        tb = t3.transpose(2, 0, 1)
        odd = x % 2 == 1
        rest = virt_col - FULL
        gap = jnp.zeros((n_virt, n_occ, EDGE - rest), BF16)
        full = jnp.where(odd, tb[:, :, rest:], tb[:, :, :FULL]).reshape(n_virt, n_occ * FULL)
        edge = jnp.where(odd, jnp.concatenate([gap, tb[:, :, :rest]], axis=2), jnp.concatenate([tb[:, :, FULL:], gap], axis=2))
        l2 = jnp.concatenate([full, edge.reshape(n_virt, n_occ * EDGE)], axis=1)
        wd3 = wd_blk.reshape(n_occ, n_virt, occ_col * n_virt)
        wx3 = wx_blk.reshape(n_occ, n_virt, occ_col * n_virt)
        start = r // 2 * 2 * n_occ + x * occ_col
        oo = jnp.stack([lax.dynamic_slice_in_dim(oooo_full, start + i * n_occ, occ_col, axis=0) for i in range(2)])
        oo = oo.reshape(2, occ_col, PLANE, 2, n_occ)
        oo = jnp.where(r % 2 == 1, oo[:, :, :, 1], oo[:, :, :, 0]).reshape(2, occ_col, PLANE * n_occ)
        ladder_sum, s1, ps = sweep_call(ts, l1, l2, vs, wd3, wx3, vvvv_blk, t_half, oo)
        s1 = s1[:, :virt_col].reshape(n_col, virt_col, occ_col, n_virt).transpose(0, 2, 1, 3).reshape(n_occ, cols_dev)
        ps = lax.dynamic_slice_in_dim(ps[:, :virt_col], PLANE * (r % EDGE), n_virt, axis=2).reshape(n_occ, cols_dev)
        ph_sym = s1 + ps
        residual = oovv_blk.astype(F32) + ladder_sum + ph_sym
        return residual / d_blk

    return jax.shard_map(local_sweep, mesh=mesh, in_specs=(amp_spec, amp_spec, amp_spec, amp_spec, P(), wide_spec, wide_spec), out_specs=amp_spec, check_vma=False)
```

time: 374 us -> 178 us (0.48)
  Pallas kernels: 0 us -> 161 us
  waiting for transfers between devices: 108 us -> 0 us
  local copies, waits for them, and re-layouts: 104 us -> 13.2 us
  matrix products: 67.7 us -> 0 us
  blocking collectives: 60 us -> 0 us
  between operations: 13.3 us -> 0.18 us
  starting transfers between devices: 7.7 us -> 0 us
  other arithmetic: 10.6 us -> 3.77 us
    pallas_call x0 -> x1, Pallas kernels: none -> 161 us  [sweep_call(): pl.pallas_call(sweep_kernel, out_shape=[jax.ShapeDtypeStruct((rows, cols)...]
    all_gather x2 -> x0, waiting for transfers between devices: 82.6 us -> none  [the longest x1 56.6 us: local_sweep(): t_cols = lax.all_gather(t_half, 'row', axis=0, tiled=True)]
    dot_general x5 -> x0, matrix products: 67.7 us -> none  [the longest x1 17.4 us: local_sweep(): lax.dot_general(hole_mat, t_half, (((0,), (0,)), ((), ())), preferred_ele...]
    reshape x4 -> x11, local copies, waits for them, and re-layouts: 71.1 us -> 6.71 us  [the longest x2 1.54 us: local_sweep(): ts = t_half.reshape(rows_dev, n_p, c_dev).transpose(1, 0, 2)]
    all_to_all x3 -> x0, blocking collectives: 60 us -> none  [the longest x1 26.7 us: local_sweep(): swap_row = lax.all_to_all(ph_back, 'row', 1, 0, tiled=True)]
    psum x1 -> x0, waiting for transfers between devices: 25.6 us -> none  [local_sweep(): x_rows = lax.psum(x_part, 'col')]
    all_to_all x9 -> x0, local copies, waits for them, and re-layouts: 20.8 us -> none  [the longest x4 10.7 us: local_sweep(): swap_both = lax.all_to_all(swap_row, 'col', 3, 2, tiled=True)]
    unnamed x13 -> x11, local copies, waits for them, and re-layouts: 8.89 us -> 1.38 us
  transfers between devices with their start and end apart: 5 -> 0, of which waited for: 3 -> 0; matrix products, arithmetic and copies ran while one was open for 42% -> 0% of each run, Pallas kernels for 0% -> 0%
where the time goes in v4:
time: 178 us
  Pallas kernels  161 us (90%)
  local copies, waits for them, and re-layouts  13.2 us (7%)
  other arithmetic  3.77 us (2%)
    pallas_call x1, Pallas kernels, sweep_call(): pl.pallas_call(sweep_kernel, out_shape=[jax.ShapeDtypeStruct((rows, cols)...  161 us

profile of v4, /device:TPU:0, one launch (start us, length us, event | category | flops | bytes accessed | tf_op | source)
XLA Modules:
  0.0 177.8 jit_solution(15465948868698767597)
XLA Ops:
  0.0 0.0 copy-start.4
  0.0 0.8 constant_dynamic-slice_fusion.1
  0.8 0.1 stack.10
  0.9 0.1 stack.9
  1.1 0.1 constant_dynamic-update-slice_fusion
  1.2 0.5 fusion
  1.6 0.0 copy-start.1
  1.7 0.7 select_n.67.oo
  2.4 0.0 copy-done.4
  2.4 0.0 copy-start
  2.4 0.7 reshape.43
  3.1 0.8 copy.30
  4.0 0.0 copy-done.1
  4.0 0.7 reshape.48
  4.7 0.8 copy.29
  5.5 0.0 copy-done
  5.5 0.8 reshape.44
  6.3 0.1 select_bitcast_fusion
  6.4 0.1 copy.23
  6.5 0.1 slice_select_fusion
  6.7 0.2 copy.22
  6.9 0.8 pad_maximum_fusion.l2
  7.6 0.1 copy.21
  7.8 0.8 reshape.45
  8.6 0.8 pad.6.l1
  9.4 160.6 %sweep.1 = (f32[32,5184]{1,0:T(8,128)}, f32[4,40,1152]{2,1,0:T(8,128)}, f32[32,40,256]{2,1,0:T(8,128)}) custom-call(bf16[8,32,648]{2,1,0:T(8,128)(2,1)} %bitcast.27, bf16[48,4608]{1,0:T(8,128)(2,1)} %pad.6.l1, bf16[144,1280]{1,0:T(8,128)(2,1)} %pad_maximum_fusion.l2, bf16[8,4,8,648]{3,2,1,0:T(8,128)(2,1)} %bitcast.28, bf16[32,144,1152]{2,1,0:T(8,128)(2,1)} %bitcast.20, ...), custom_call_target="tpu_custom_call" | custom-call | tf_op jit(solution)/shard_map/sweep/pallas_call | solution.py:455
  170.0 1.3 copy.25
  171.2 0.8 reshape.51
  172.1 0.7 copy.26
  172.8 0.0 copy-start.3
  172.8 0.5 reshape.52
  173.3 0.8 copy-done.3
  174.1 0.4 constant_dynamic-slice_fusion
  174.5 0.0 copy-start.2
  174.5 0.5 reshape.53
  175.0 0.5 copy-done.2
  175.5 2.3 %add_divide_fusion = f32[32,5184]{1,0:T(8,128)} fusion(f32[32,5184]{1,0:T(8,128)} %param.8, f32[32,5184]{1,0:T(8,128)S(1)} %reshape.52, f32[32,5184]{1,0:T(8,128)S(1)} %reshape.53, f32[32,5184]{1,0:T(8,128)} %get-tuple-element.8, bf16[32,5184]{1,0:T(8,128)(2,1)S(1)} %copy-done.2), kind=kLoop, calls=%fused_computation | loop fusion | flops 829440 | bytes 3649536 | tf_op jit(solution)/shard_map/div | solution.py:519
  (3 shorter events, 0.1 us)
Async XLA Ops:
  0.0 2.4 %copy-start.4 = (f32[32,5184]{1,0:T(8,128)S(1)}, f32[32,5184]{1,0:T(8,128)}, u32[]{:S(2)}) copy-start(f32[32,5184]{1,0:T(8,128)} %param.7) | copy-start | bytes 1990660
  1.6 2.3 %copy-start.1 = (bf16[32,5184]{1,0:T(8,128)(2,1)S(1)}, bf16[32,5184]{1,0:T(8,128)(2,1)}, u32[]{:S(2)}) copy-start(bf16[32,5184]{1,0:T(8,128)(2,1)} %param.9) | copy-start | bytes 995332
  2.4 3.1 %copy-start = (bf16[32,5184]{1,0:T(8,128)(2,1)}, bf16[32,5184]{1,0:T(8,128)(2,1)S(1)}, u32[]{:S(2)}) copy-start(bf16[32,5184]{1,0:T(8,128)(2,1)S(1)} %convert_element_type.9.t2) | copy-start | bytes 995332
  172.8 1.3 copy-start.3
  174.5 1.0 copy-start.2

commit v5 on v4

--- a/solution.py
+++ b/solution.py
@@ -17,6 +17,7 @@
 FULL = 32
 EDGE = 8
 N_CH = 10
+EARLY = 3
 CW = 512
 TAIL = 64
 
@@ -51,11 +52,11 @@
     pl.semaphore_wait(bar, RING - 1 + ROWS - 1 + RING * (RING - 1))
 
 
-def sweep_kernel(ts, l1, l2, vs, wd, wx, v_hbm, t2, oo, out, s1_in, ps_in,
-                 g, tl, vl, lg1, lg2, wdb, wxb, wxs, d_n, e_n, sw, s2_in, v_buf, t_pair, m_t, x_part, x_in, m_all,
+def sweep_kernel(ts, l1, l2, vs, wd, wx, v_hbm, t2, oo_hbm, out_hbm,
+                 g, tl, vl, lg1, lg2, wdb, wxb, wxs, d_n, e_n, s_f, s_b, sw, s1_in, s2_in, ps_in, out, oo2, oo, v_buf, t_pair, m_t, x_part, x_in, m_all,
                  p_b, p_t, r1, r1t, r2, r2t,
                  g_s, g_r, t_s, t_r, p_s, p_r, o_s, o_r, v_s, v_r, f_s, f_r, loc, wd_s, wx_s, wy_s,
-                 vl_s, vx_s, vx_r, tp_s, tp_r, x_s, x_r, m_s, m_r, s1, w1, s2, w2, sw_s, sw_r, ps_s, ps_r):
+                 vl_s, vx_s, vx_r, tp_s, tp_r, x_s, x_r, m_s, m_r, s1, w1, s2, w2, sw_s, sw_r, ps_s, ps_r, out_s, oo_s):
     x, z, y, core, q, r = _place()
     right, left = (x + 1) % RING, (x + RING - 1) % RING
     mate = (x, q * 2 + 1 - core)
@@ -89,7 +90,7 @@
     own2.start()
 
     def wd_copy(i):
-        return pltpu.make_async_copy(wd.at[pl.ds(EDGE * i, EDGE)], wdb.at[i % 2], wd_s.at[i % 2])
+        return pltpu.make_async_copy(wd.at[pl.ds(RING * i, RING)], wdb.at[i % 2], wd_s.at[i % 2])
 
     def wx_copy(i):
         c, h = i // 2, n_kd // 2
@@ -99,7 +100,12 @@
     def wy_copy(i):
         return pltpu.make_async_copy(wx.at[:, pl.ds(FULL + n_v // 2 * i, EDGE)], wxs.at[i], wy_s.at[i])
 
+    def oo_copy(i):
+        k0 = pl.multiple_of((2 * q + i) * rows + x * EDGE, EDGE)
+        return pltpu.make_async_copy(oo_hbm.at[pl.ds(k0, EDGE)], oo2.at[i], oo_s.at[i])
+
     for i in range(2):
+        oo_copy(i).start()
         wd_copy(i).start()
         wx_copy(i).start()
         wy_copy(i).start()
@@ -141,7 +147,6 @@
 
     own.wait()
     t_block(0)
-    v_each(lambda c: c.start(), v_own.start)
     g0.wait_recv()
     g2 = g2()
     g2.start()
@@ -149,6 +154,7 @@
     g1.wait_recv()
     g3 = g3()
     g3.start()
+    v_each(lambda c: c.start(), v_own.start)
     t_block(1)
     a0, a1, a2, a3 = ring(l1, lg1, p_s, p_r, 1)
     b0, b1, b2, b3 = ring(l2, lg2, o_s, o_r, 1)
@@ -170,37 +176,45 @@
     for c in v_in:
         c.start()
 
+    for i in range(2):
+        oo_copy(i).wait()
+    ow = oo2[...].astype(F32)
+    for k in range(PLANE):
+        c0 = 2 * k * rows
+        oo[:, :, k * rows:(k + 1) * rows] = jnp.where(core == 1, ow[:, :, c0 + rows:c0 + 2 * rows], ow[:, :, c0:c0 + rows])
+
     pl.when(x == z)(v_own.wait)
     pl.when(x != z)(lambda: v_arrival(0).wait_recv())
     for k in range(1, PLANE):
         v_arrival(k).wait_recv()
     fwd = _rc(vl.at[:, core], vl.at[:, core], f_s, f_r, mate)
     fwd.start()
+
+    pltpu.make_async_copy(g.at[x, pl.ds(2 * y, 2)], tl.at[:, q], loc_t).wait()
+    for k in range(1, PLANE):
+        t_arrival(k).wait_recv()
+    fwd.wait()
+
+    k8 = vl.shape[3]
+    n_i = PLANE * rows
+    n_k = 2 * PLANE * k8
+    dn = (((1,), (1,)), ((), ()))
+    xp = [lax.dot_general(vl[i].reshape(n_k, n_c), tl[i].reshape(n_i, n_c), dn, preferred_element_type=F32) for i in range(2)]
+    x_part[...] = (xp[0] + xp[1]).reshape(2, PLANE, k8, n_i)
+
+    def x_copy(k):
+        qd = (q + k) % PLANE
+        return _rc(x_part.at[:, qd], x_in.at[q], x_s.at[k], x_r.at[k], (x, qd * 2 + core))
+
+    for k in range(1, PLANE):
+        x_copy(k).start()
+    x_in[q] = x_part[:, q]
     a0.wait_recv()
     a2 = a2()
     a2.start()
     a1.wait_recv()
     a3 = a3()
     a3.start()
-    pltpu.make_async_copy(g.at[x, pl.ds(2 * y, 2)], tl.at[:, q], loc_t).wait()
-    for k in range(1, PLANE):
-        t_arrival(k).wait_recv()
-    fwd.wait()
-
-    k8 = vl.shape[3]
-    n_i = PLANE * rows
-    n_k = 2 * PLANE * k8
-    dn = (((1,), (1,)), ((), ()))
-    xp = [lax.dot_general(vl[i].reshape(n_k, n_c), tl[i].reshape(n_i, n_c), dn, preferred_element_type=F32) for i in range(2)]
-    x_part[...] = (xp[0] + xp[1]).reshape(2, PLANE, k8, n_i)
-
-    def x_copy(k):
-        qd = (q + k) % PLANE
-        return _rc(x_part.at[:, qd], x_in.at[q], x_s.at[k], x_r.at[k], (x, qd * 2 + core))
-
-    for k in range(1, PLANE):
-        x_copy(k).start()
-    x_in[q] = x_part[:, q]
     b0.wait_recv()
     b2 = b2()
     b2.start()
@@ -208,87 +222,92 @@
     b3 = b3()
     b3.start()
 
-    n1 = l1.shape[0]
-    quarter = n_v // RING
-    own1.wait()
-    own2.wait()
-    a2.wait_recv()
-    a3.wait_recv()
-    acc = None
-    for i in range(RING):
-        wd_copy(i).wait()
-        lhs = lg1[:, :, i * EDGE * n_v:(i + 1) * EDGE * n_v].reshape(RING * n1, EDGE * n_v)
-        d = jnp.dot(lhs, wdb[i % 2].reshape(EDGE * n_v, n_j), preferred_element_type=F32)
-        acc = d if acc is None else acc + d
-        if i < 2:
-            wd_copy(i + 2).start()
-    for i in range(RING):
-        d_n[quarter * i:quarter * (i + 1), :] = acc[n1 * i:n1 * i + quarter]
-    b2.wait_recv()
-    b3.wait_recv()
-    acc = None
-    kb = FULL * n_kd
-    kh = kb // 2
-    for i in range(2 * RING):
-        wx_copy(i).wait()
-        d = jnp.dot(lg2[i // 2, :, i % 2 * kh:(i % 2 + 1) * kh], wxb[i % 2].reshape(kh, n_j), preferred_element_type=F32)
-        acc = d if acc is None else acc + d
-        if i + 2 < 2 * RING:
-            wx_copy(i + 2).start()
-    for i in range(2):
-        wy_copy(i).wait()
-        lhs = lg2[2 * i, :, kb:] + lg2[2 * i + 1, :, kb:]
-        acc = acc + jnp.dot(lhs, wxs[i].reshape(EDGE * n_kd, n_j), preferred_element_type=F32)
-    e_n[...] = acc
-
     for k in range(1, PLANE):
         x_copy(k).wait_recv()
     xs = x_in[0]
     for k in range(1, PLANE):
         xs = xs + x_in[k]
-    m_all[x] = (oo[...].astype(F32) + 0.5 * xs).astype(BF16)
+    m_all[x] = (oo[...] + 0.5 * xs).astype(BF16)
 
     def m_copy(k):
         return _rc(m_all.at[x], m_all.at[x], m_s.at[k], m_r.at[k], ((x + k) % RING, r))
 
     for k in range(1, RING):
         m_copy(k).start()
-
-    for j in range(n_j // n_v):
-        cut = slice(j * n_v, (j + 1) * n_v)
-        sj = d_n[:, cut] - e_n[:, cut].T
-        d_n[:, cut] = sj
-        e_n[:, cut] = sj.T
-    for i in range(RING):
-        sw[0, i, :quarter, :] = d_n[quarter * i:quarter * (i + 1), :]
-        sw[1, i, :quarter, :] = e_n[quarter * i:quarter * (i + 1), :]
 
     def s_copy(i, k):
         xd = (x + k) % RING
         return _rc(sw.at[i, xd], (s1_in, s2_in)[i].at[x], sw_s.at[i, k], sw_r.at[i, k], (xd, r))
 
     s_own = [pltpu.make_async_copy(sw.at[i, x], (s1_in, s2_in)[i].at[x], (loc_a, loc_b)[i]) for i in range(2)]
-    for i in (1, 0):
-        for k in range(1, RING):
-            s_copy(i, k).start()
-        s_own[i].start()
-
     def ps_src(rd):
-        return s2_in.at[rd // EDGE, :, pl.ds(pl.multiple_of(rd % EDGE * 9 // EDGE * LANE, LANE), 2 * LANE)]
+        return s2_in.at[rd // EDGE, pl.ds(rd % EDGE, 1)]
 
     def ps_copy(k):
         rd = (r + k) % ROWS
-        return _rc(ps_src(rd), ps_in.at[r], ps_s.at[k], ps_r.at[k], (x, rd))
-
-    ps_own = pltpu.make_async_copy(ps_src(r), ps_in.at[r], loc_g)
-
-    def ps_send():
+        return _rc(ps_src(rd), ps_in.at[pl.ds(r, 1)], ps_s.at[k], ps_r.at[k], (x, rd))
+
+    ps_own = pltpu.make_async_copy(ps_src(r), ps_in.at[pl.ds(r, 1)], loc_g)
+
+    def ps_ready():
         s_own[1].wait()
         for k in range(1, RING):
             s_copy(1, k).wait_recv()
         ps_own.start()
-        for k in range(1, ROWS):
+
+    def ps_send(lo, hi):
+        for k in range(lo, hi):
             ps_copy(k).start()
+
+    def s_work():
+        n1 = l1.shape[0]
+        quarter = n_v // RING
+        own1.wait()
+        own2.wait()
+        a2.wait_recv()
+        a3.wait_recv()
+        acc = None
+        kd = RING * n_v
+        for i in range(2 * RING):
+            wd_copy(i).wait()
+            lhs = lg1[:, :, i * kd:(i + 1) * kd].reshape(RING * n1, kd)
+            d = jnp.dot(lhs, wdb[i % 2].reshape(kd, n_j), preferred_element_type=F32)
+            acc = d if acc is None else acc + d
+            if i + 2 < 2 * RING:
+                wd_copy(i + 2).start()
+        for i in range(RING):
+            d_n[quarter * i:quarter * (i + 1), :] = acc[n1 * i:n1 * i + quarter]
+        b2.wait_recv()
+        b3.wait_recv()
+        acc = None
+        kb = FULL * n_kd
+        kh = kb // 2
+        for i in range(2 * RING):
+            wx_copy(i).wait()
+            d = jnp.dot(lg2[i // 2, :, i % 2 * kh:(i % 2 + 1) * kh], wxb[i % 2].reshape(kh, n_j), preferred_element_type=F32)
+            acc = d if acc is None else acc + d
+            if i + 2 < 2 * RING:
+                wx_copy(i + 2).start()
+        for i in range(2):
+            wy_copy(i).wait()
+            lhs = lg2[2 * i, :, kb:] + lg2[2 * i + 1, :, kb:]
+            acc = acc + jnp.dot(lhs, wxs[i].reshape(EDGE * n_kd, n_j), preferred_element_type=F32)
+        e_n[...] = acc
+
+        for j in range(n_j // n_v):
+            cut = slice(j * n_v, (j + 1) * n_v)
+            sj = d_n[:, cut] - e_n[:, cut].T
+            s_f[j] = sj
+            s_b[j] = sj.T
+        for i in range(2):
+            for a in range(n_v):
+                c0 = a % quarter * n_v
+                sw[i, a // quarter, :, c0:c0 + n_v] = (s_f, s_b)[i][:, a, :]
+        for i in (1, 0):
+            for k in range(1, RING):
+                s_copy(i, k).start()
+            s_own[i].start()
+
 
     for c in v_in:
         c.wait()
@@ -356,14 +375,19 @@
         for i in range(4):
             nxt(i).start()
 
+    def o_copy(t, c0, w):
+        return pltpu.make_async_copy(out.at[:, pl.ds(c0, w)], out_hbm.at[:, pl.ds(c0, w)], out_s.at[t])
+
     def l5_step(t, a, pb, rb, rb2, c0, w):
         u, v = coords(a)
         h = rows // 2
         msg, old = stage(False, t, a, pb, rb2), stage(True, t, a, pb, rb)
         for i in near:
             msg(i).wait_recv()
-        out[:h, pl.ds(c0, w)] = pb[u, v, :h] + rb2[4] + rb2[3]
-        out[h:, pl.ds(c0, w)] = pb[u, v, h:] + rb2[2] + rb2[5]
+        sym = s1_in[:, :, pl.ds(c0, w)].reshape(rows, w) + ps_in[:, pl.ds(c0, w)]
+        out[:h, pl.ds(c0, w)] = pb[u, v, :h] + rb2[4] + rb2[3] + sym[:h]
+        out[h:, pl.ds(c0, w)] = pb[u, v, h:] + rb2[2] + rb2[5] + sym[h:]
+        o_copy(t, c0, w).start()
         for i in range(6):
             msg(i).wait_send()
             old(i).wait_send()
@@ -374,34 +398,62 @@
     def col0(t):
         return pl.multiple_of((t // 2) * CW + (t % 2) * (N_CH // 2) * CW, LANE)
 
-    def loop(lo, fn):
-        lax.fori_loop(lo, N_CH, lambda t, c: (fn(t), c)[1], 0)
+    def loop(lo, fn, hi=N_CH):
+        lax.fori_loop(lo, hi, lambda t, c: (fn(t), c)[1], 0)
 
     tail = (N_CH, 1, p_t, r1t, r2t)
     ct = N_CH * CW
+
+    def each(p, fn):
+        for i in range(2):
+            fn(2 * p + i)
 
     def run1(t):
         n, a, pb, rb, _ = at(t)
         l1_step(n, a, pb, rb, col0(t), CW)
 
+    def run2(t):
+        add_step(True, *at(t)[:4])
+
     def run3(t):
         l3_step(*at(t))
-        n, a, pb, _, rb2 = at(t - 1)
+
+    def run4(t):
+        n, a, pb, _, rb2 = at(t)
         add_step(False, n, a, pb, rb2)
 
+    pairs = N_CH // 2
+    loop(0, run1, 2 * EARLY)
     l1_step(*tail[:4], ct, TAIL)
-    loop(0, run1)
-    ps_send()
+    s_work()
     add_step(True, *tail[:4])
-    loop(0, lambda t: add_step(True, *at(t)[:4]))
+
+    def pair_step(p):
+        each(p, run2)
+        pl.when(p + EARLY < pairs)(lambda: each(p + EARLY, run1))
+        pl.when(p >= 1)(lambda: each(p - 1, run3))
+        pl.when(p >= 2)(lambda: each(p - 2, run4))
+
+    lax.fori_loop(0, pairs, lambda p, c: (pair_step(p), c)[1], 0)
+    ps_ready()
+    ps_send(1, 12)
     l3_step(*tail)
+    each(pairs - 2, run4)
+    each(pairs - 1, run3)
     add_step(False, *tail[:3], r2t)
-    l3_step(*at(0))
-    loop(1, run3)
-    n, a, pb, _, rb2 = at(N_CH - 1)
-    add_step(False, n, a, pb, rb2)
+    ps_send(12, 22)
+    each(pairs - 1, run4)
+    ps_send(22, ROWS)
+    s_own[0].wait()
+    ps_own.wait()
+    for k in range(1, RING):
+        s_copy(0, k).wait_recv()
+    for k in range(1, ROWS):
+        ps_copy(k).wait_recv()
     l5_step(*tail, ct, TAIL)
     loop(0, lambda t: l5_step(*at(t), col0(t), CW))
+    for i in range(N_CH + 1):
+        o_copy(i, i * CW, CW if i < N_CH else TAIL).wait()
 
     for c in (g0, g1, g2, g3, a0, a1, a2, a3, b0, b1, b2, b3):
         c.wait_send()
@@ -418,12 +470,10 @@
         x_copy(k).wait_send()
     for k in range(1, RING):
         m_copy(k).wait_send()
-        s_copy(0, k).wait()
+        s_copy(0, k).wait_send()
         s_copy(1, k).wait_send()
-    s_own[0].wait()
-    ps_own.wait()
     for k in range(1, ROWS):
-        ps_copy(k).wait()
+        ps_copy(k).wait_send()
 
 
 def sweep_call(ts, l1, l2, vs, wd, wx, v, t2, oo):
@@ -432,7 +482,7 @@
     cols = t2.shape[1]
     k8 = rows // RING
     n_i = PLANE * rows
-    blk = (n_v // RING + RING, n_j)
+    blk = (RING, k8, cols)
     n = N_CH + 1
     dma = pltpu.SemaphoreType.DMA
     vm = pl.BlockSpec(memory_space=pltpu.VMEM)
@@ -451,21 +501,17 @@
     all16, sq = (PLANE,), (RING, RING)
     v9 = (-(-cols // 640),)
     counts = [four, four, sq, all16, four, four, four, four, sq, all16, one, one, (8,), two, two, two,
-              v9, v9, v9, one, one, all16, all16, four, four, six, six, six, six, (2, RING), (2, RING), (ROWS,), (ROWS,)]
+              v9, v9, v9, one, one, all16, all16, four, four, six, six, six, six, (2, RING), (2, RING), (ROWS,), (ROWS,), (n,), two]
     return pl.pallas_call(
         sweep_kernel,
-        out_shape=[
-            jax.ShapeDtypeStruct((rows, cols), F32),
-            jax.ShapeDtypeStruct((RING,) + blk, F32),
-            jax.ShapeDtypeStruct((ROWS, blk[0], 2 * LANE), F32),
-        ],
-        in_specs=[vm, vm, vm, vm, hbm, hbm, hbm, vm, vm],
-        out_specs=[vm, vm, vm],
+        out_shape=jax.ShapeDtypeStruct((rows, cols), F32),
+        in_specs=[vm, vm, vm, vm, hbm, hbm, hbm, vm, hbm],
+        out_specs=hbm,
         scratch_shapes=[
             b16(RING, n_p, rows, n_c), b16(2, PLANE, rows, n_c), b16(2, 2, PLANE, k8, n_c),
             b16(RING, *l1.shape), b16(RING, *l2.shape),
-            b16(2, EDGE, n_v, n_j), b16(2, n_k // 2, FULL, n_j), b16(2, n_k, EDGE, n_j),
-            f32(n_v, n_j), f32(n_v, n_j), f32(2, RING, *blk), f32(RING, *blk),
+            b16(2, RING, n_v, n_j), b16(2, n_k // 2, FULL, n_j), b16(2, n_k, EDGE, n_j),
+            f32(n_v, n_j), f32(n_v, n_j), f32(k8, n_v, n_v), f32(k8, n_v, n_v), f32(2, *blk), f32(*blk), f32(*blk), f32(rows, cols), f32(rows, cols), b16(2, k8, 2 * n_i), f32(2, k8, n_i),
             b16(2, n_c, cols), b16(2, rows, cols), b16(n_i, 2 * rows),
             f32(2, PLANE, k8, n_i), f32(PLANE, 2, k8, n_i), b16(RING, 2, k8, n_i),
             f32(N_CH, RING, RING, rows, CW), f32(RING, RING, rows, TAIL),
@@ -491,7 +537,6 @@
         c_dev = vvvv_blk.shape[0]
         n_p = cols_dev // c_dev
         x = lax.axis_index("col")
-        r = lax.axis_index("row")
         t_half = t_blk.astype(BF16)
         ts = t_half.reshape(rows_dev, n_p, c_dev).transpose(1, 0, 2)
         vs = oovv_blk.reshape(n_col, occ_col, n_p, c_dev).transpose(2, 0, 1, 3)
@@ -507,15 +552,7 @@
         l2 = jnp.concatenate([full, edge.reshape(n_virt, n_occ * EDGE)], axis=1)
         wd3 = wd_blk.reshape(n_occ, n_virt, occ_col * n_virt)
         wx3 = wx_blk.reshape(n_occ, n_virt, occ_col * n_virt)
-        start = r // 2 * 2 * n_occ + x * occ_col
-        oo = jnp.stack([lax.dynamic_slice_in_dim(oooo_full, start + i * n_occ, occ_col, axis=0) for i in range(2)])
-        oo = oo.reshape(2, occ_col, PLANE, 2, n_occ)
-        oo = jnp.where(r % 2 == 1, oo[:, :, :, 1], oo[:, :, :, 0]).reshape(2, occ_col, PLANE * n_occ)
-        ladder_sum, s1, ps = sweep_call(ts, l1, l2, vs, wd3, wx3, vvvv_blk, t_half, oo)
-        s1 = s1[:, :virt_col].reshape(n_col, virt_col, occ_col, n_virt).transpose(0, 2, 1, 3).reshape(n_occ, cols_dev)
-        ps = lax.dynamic_slice_in_dim(ps[:, :virt_col], PLANE * (r % EDGE), n_virt, axis=2).reshape(n_occ, cols_dev)
-        ph_sym = s1 + ps
-        residual = oovv_blk.astype(F32) + ladder_sum + ph_sym
-        return residual / d_blk
+        summed = sweep_call(ts, l1, l2, vs, wd3, wx3, vvvv_blk, t_half, oooo_full)
+        return (oovv_blk.astype(F32) + summed) / d_blk
 
     return jax.shard_map(local_sweep, mesh=mesh, in_specs=(amp_spec, amp_spec, amp_spec, amp_spec, P(), wide_spec, wide_spec), out_specs=amp_spec, check_vma=False)

time: 178 us -> 152 us (0.85)
  Pallas kernels: 161 us -> 140 us
  local copies, waits for them, and re-layouts: 13.2 us -> 5.88 us
    pallas_call x1, Pallas kernels: 161 us -> 140 us  [sweep_call(): pl.pallas_call(sweep_kernel, out_shape=jax.ShapeDtypeStruct((rows, cols),...]
where the time goes in v5:
time: 152 us; the launch traced here: 151 us
  Pallas kernels  140 us (92%)
  local copies, waits for them, and re-layouts  5.88 us (4%)
  other arithmetic  4.48 us (3%)
    pallas_call x1, Pallas kernels, sweep_call(): pl.pallas_call(sweep_kernel, out_shape=jax.ShapeDtypeStruct((rows, cols),...  140 us

profile of v5, /device:TPU:0, one launch (start us, length us, event | category | flops | bytes accessed | tf_op | source)
XLA Modules:
  0.0 150.5 jit_solution(7419864566674901637)
XLA Ops:
  0.0 0.0 copy-start.1
  0.0 1.2 convert_element_type.9.t2
  1.2 0.0 copy-start
  1.2 0.8 reshape.25
  2.0 0.1 select_bitcast_fusion
  2.1 0.1 copy.15
  2.2 0.1 slice_select_fusion
  2.4 0.2 copy.14
  2.5 0.8 pad_maximum_fusion.l2
  3.3 0.1 copy.13
  3.4 0.8 reshape.26
  4.3 0.8 pad.6.l1
  5.1 0.0 copy-done
  5.1 0.7 reshape.24
  5.8 0.8 copy.20
  6.6 0.0 copy-done.1
  6.6 0.7 reshape.29
  7.3 0.8 copy.19
  8.1 140.1 %sweep.1 = f32[32,5184]{1,0:T(8,128)} custom-call(bf16[8,32,648]{2,1,0:T(8,128)(2,1)} %bitcast.19, bf16[48,4608]{1,0:T(8,128)(2,1)} %pad.6.l1, bf16[144,1280]{1,0:T(8,128)(2,1)} %pad_maximum_fusion.l2, bf16[8,4,8,648]{3,2,1,0:T(8,128)(2,1)} %bitcast.20, bf16[32,144,1152]{2,1,0:T(8,128)(2,1)} %bitcast.13, bf16[32,144,1152]{2,1,0:T(8,128)(2,1)} %bitcast.14, ...), custom_call_target="tpu_custom_call" | custom-call | tf_op jit(solution)/shard_map/sweep/pallas_call | solution.py:505
  148.2 2.3 %add_divide_fusion = f32[32,5184]{1,0:T(8,128)} fusion(f32[32,5184]{1,0:T(8,128)} %param.8, f32[32,5184]{1,0:T(8,128)} %sweep.1, bf16[32,5184]{1,0:T(8,128)(2,1)} %param.9), kind=kLoop, calls=%fused_computation | loop fusion | flops 497664 | bytes 2322432 | tf_op jit(solution)/shard_map/div | solution.py:556
  (1 shorter events, 0.0 us)
Async XLA Ops:
  0.0 6.6 %copy-start.1 = (bf16[32,5184]{1,0:T(8,128)(2,1)S(1)}, bf16[32,5184]{1,0:T(8,128)(2,1)}, u32[]{:S(2)}) copy-start(bf16[32,5184]{1,0:T(8,128)(2,1)} %param.9) | copy-start | bytes 995332
  1.2 3.9 %copy-start = (bf16[32,5184]{1,0:T(8,128)(2,1)}, bf16[32,5184]{1,0:T(8,128)(2,1)S(1)}, u32[]{:S(2)}) copy-start(bf16[32,5184]{1,0:T(8,128)(2,1)S(1)} %convert_element_type.9.t2) | copy-start | bytes 995332

commit v6 on v5

--- a/solution.py
+++ b/solution.py
@@ -17,7 +17,7 @@
 FULL = 32
 EDGE = 8
 N_CH = 10
-EARLY = 3
+EARLY = 5
 CW = 512
 TAIL = 64
 
@@ -33,7 +33,7 @@
     return pltpu.make_async_remote_copy(src_ref=src, dst_ref=dst, send_sem=ssem, recv_sem=rsem, device_id=dev, device_id_type=MESH)
 
 
-def _enter(x, z, core, r):
+def _enter(x, r):
     bar = pltpu.get_barrier_semaphore()
 
     def tell(dev):
@@ -44,26 +44,22 @@
     for k in range(1, ROWS):
         tell((x, (r + k) % ROWS))
 
-    @pl.when(x != z)
-    def _():
-        for k in range(PLANE):
-            tell((z, k * 2 + core))
-
-    pl.semaphore_wait(bar, RING - 1 + ROWS - 1 + RING * (RING - 1))
-
-
-def sweep_kernel(ts, l1, l2, vs, wd, wx, v_hbm, t2, oo_hbm, out_hbm,
-                 g, tl, vl, lg1, lg2, wdb, wxb, wxs, d_n, e_n, s_f, s_b, sw, s1_in, s2_in, ps_in, out, oo2, oo, v_buf, t_pair, m_t, x_part, x_in, m_all,
+    pl.semaphore_wait(bar, RING - 1 + ROWS - 1)
+
+
+def sweep_kernel(tv, l1, l2, wd, wx, v_hbm, t2, oo_hbm, out_hbm,
+                 h_in, hv, vo, tl, lg1, lg2, wdb, wxb, wxs, d_n, e_n, s_f, s_b, sw, s1_in, s2_in, ps_in, out, oo2, oo, v_buf, t_pair, m_t, x_part, x_in, m_all,
                  p_b, p_t, r1, r1t, r2, r2t,
-                 g_s, g_r, t_s, t_r, p_s, p_r, o_s, o_r, v_s, v_r, f_s, f_r, loc, wd_s, wx_s, wy_s,
+                 g_s, g_r, h_s, h_r, t_s, t_r, p_s, p_r, o_s, o_r, f_s, f_r, loc, wd_s, wx_s, wy_s,
                  vl_s, vx_s, vx_r, tp_s, tp_r, x_s, x_r, m_s, m_r, s1, w1, s2, w2, sw_s, sw_r, ps_s, ps_r, out_s, oo_s):
     x, z, y, core, q, r = _place()
     right, left = (x + 1) % RING, (x + RING - 1) % RING
     mate = (x, q * 2 + 1 - core)
     n_kd, n_v, n_j = wd.shape
-    rows, n_c = tl.shape[2:]
+    k8, n_c = tl.shape[3:]
+    rows = RING * k8
     loc_g, loc_t, loc_1, loc_2, loc_v, loc_p, loc_a, loc_b = [loc.at[i] for i in range(loc.shape[0])]
-    _enter(x, z, core, r)
+    _enter(x, r)
 
     def ring(src, buf, ss, rr, axis):
         h = src.shape[axis] // 2
@@ -79,15 +75,25 @@
         c1 = _rc(src, buf.at[x], ss.at[1], rr.at[1], (left, r))
         return c0, c1, lambda: hop(2, r, left, right), lambda: hop(3, r, right, left)
 
-    own = pltpu.make_async_copy(ts, g.at[x], loc_g)
     own1 = pltpu.make_async_copy(l1, lg1.at[x], loc_1)
     own2 = pltpu.make_async_copy(l2, lg2.at[x], loc_2)
-    g0, g1, g2, g3 = ring(ts, g, g_s, g_r, 0)
-    own.start()
-    g0.start()
-    g1.start()
+    def h_copy(k):
+        xd = (x + k) % RING
+        return _rc(tv.at[xd], h_in.at[x], h_s.at[k], h_r.at[k], (xd, r))
+
+    for k in (1, RING - 1, 2):
+        h_copy(k).start()
     own1.start()
     own2.start()
+
+    def onward(r0, r1_, f0, f1):
+        r0.wait_recv()
+        f0 = f0()
+        f0.start()
+        r1_.wait_recv()
+        f1 = f1()
+        f1.start()
+        return [f0, f1]
 
     def wd_copy(i):
         return pltpu.make_async_copy(wd.at[pl.ds(RING * i, RING)], wdb.at[i % 2], wd_s.at[i % 2])
@@ -110,59 +116,34 @@
         wx_copy(i).start()
         wy_copy(i).start()
 
-    def v_copy(x2, yd):
-        return _rc(vs.at[pl.ds(2 * yd, 2), x2], vl.at[:, core, q], v_s.at[x2, yd], v_r.at[q], (x2, (x * RING + yd) * 2 + core))
-
-    def v_arrival(k):
-        return _rc(vs.at[pl.ds(2 * y, 2), x], vl.at[:, core, (q + k) % PLANE], v_s.at[x, y], v_r.at[(q + k) % PLANE], (x, r))
-
-    v_own = pltpu.make_async_copy(vs.at[pl.ds(2 * y, 2), x], vl.at[:, core, q], loc_v)
-
-    def v_each(act, act_own):
-        for i in range(RING):
-            for k in range(RING):
-                c = v_copy((x + i) % RING, (y + k) % RING)
-                if i + k == 0:
-                    if act_own is not None:
-                        pl.when(x == z)(act_own)
-                    pl.when(x != z)(lambda: act(c))
-                else:
-                    act(c)
-
-    def t_copy(xs, yd):
-        return _rc(g.at[xs, pl.ds(2 * yd, 2)], tl.at[:, q], t_s.at[xs, yd], t_r.at[q], (x, (xs * RING + yd) * 2 + core))
-
-    def t_arrival(k):
-        return _rc(g.at[x, pl.ds(2 * y, 2)], tl.at[:, (q + k) % PLANE], t_s.at[x, y], t_r.at[(q + k) % PLANE], (x, r))
+    def piece(xs, yd, buf):
+        return buf.at[xs, pl.ds(2 * yd, 2)]
+
+    def t_copy(xs, yd, buf):
+        return _rc(piece(xs, yd, buf), hv.at[:, :, q], t_s, t_r, (x, (xs * RING + yd) * 2 + core))
+
+    def t_own(xs, buf):
+        return pltpu.make_async_copy(piece(xs, y, buf), hv.at[:, :, q], loc_t)
 
     def t_block(rel):
         xs = (x + rel) % RING
+        buf = tv if rel == 0 else h_in
         for k in range(RING):
             yd = (y + k) % RING
             if k == 0:
-                pl.when(xs == z)(lambda: pltpu.make_async_copy(g.at[xs, pl.ds(2 * yd, 2)], tl.at[:, q], loc_t).start())
-                pl.when(xs != z)(lambda: t_copy(xs, yd).start())
+                pl.when(xs == z)(lambda: t_own(xs, buf).start())
+                pl.when(xs != z)(lambda: t_copy(xs, yd, buf).start())
             else:
-                t_copy(xs, yd).start()
-
-    own.wait()
+                t_copy(xs, yd, buf).start()
+
     t_block(0)
-    g0.wait_recv()
-    g2 = g2()
-    g2.start()
-    t_block(RING - 1)
-    g1.wait_recv()
-    g3 = g3()
-    g3.start()
-    v_each(lambda c: c.start(), v_own.start)
-    t_block(1)
     a0, a1, a2, a3 = ring(l1, lg1, p_s, p_r, 1)
     b0, b1, b2, b3 = ring(l2, lg2, o_s, o_r, 1)
-    for c in (a0, a1, b0, b1):
-        c.start()
-    g2.wait_recv()
-    g3.wait_recv()
-    t_block(2)
+    a0.start()
+    a1.start()
+    for k in (1, RING - 1, 2):
+        h_copy(k).wait_recv()
+        t_block(RING - k)
 
     n_v9 = vl_s.shape[0]
     wide = 640
@@ -182,48 +163,56 @@
     for k in range(PLANE):
         c0 = 2 * k * rows
         oo[:, :, k * rows:(k + 1) * rows] = jnp.where(core == 1, ow[:, :, c0 + rows:c0 + 2 * rows], ow[:, :, c0:c0 + rows])
-
-    pl.when(x == z)(v_own.wait)
-    pl.when(x != z)(lambda: v_arrival(0).wait_recv())
-    for k in range(1, PLANE):
-        v_arrival(k).wait_recv()
-    fwd = _rc(vl.at[:, core], vl.at[:, core], f_s, f_r, mate)
+    ot = oo[...].reshape(2 * k8, PLANE * rows).T
+    ot = jnp.concatenate([ot[k * rows + i * k8:k * rows + (i + 1) * k8] for i in range(RING) for k in range(PLANE)], axis=0)
+    oo[...] = ot.T.reshape(2, k8, PLANE * rows)
+
+    t_own(x, tv).wait()
+    t_others = hv.at[:, :, pl.ds(0, PLANE - 1)]
+    pltpu.make_async_copy(t_others, t_others, t_r).wait()
+    g0, g1, g2, g3 = ring(hv.at[:, 0], tl, g_s, g_r, 0)
+    g0.start()
+    g1.start()
+    fwd = _rc(hv.at[:, 1], vo, f_s, f_r, mate)
     fwd.start()
-
-    pltpu.make_async_copy(g.at[x, pl.ds(2 * y, 2)], tl.at[:, q], loc_t).wait()
-    for k in range(1, PLANE):
-        t_arrival(k).wait_recv()
+    own = pltpu.make_async_copy(hv.at[:, 0], tl.at[x], loc_g)
+    own.start()
+    g0.wait_recv()
+    g2 = g2()
+    g2.start()
+    g1.wait_recv()
+    g3 = g3()
+    g3.start()
+    a_fwd = onward(a0, a1, a2, a3)
     fwd.wait()
-
-    k8 = vl.shape[3]
+    own.wait()
+    g2.wait_recv()
+    g3.wait_recv()
+
     n_i = PLANE * rows
-    n_k = 2 * PLANE * k8
+    n_k = PLANE * k8
     dn = (((1,), (1,)), ((), ()))
-    xp = [lax.dot_general(vl[i].reshape(n_k, n_c), tl[i].reshape(n_i, n_c), dn, preferred_element_type=F32) for i in range(2)]
-    x_part[...] = (xp[0] + xp[1]).reshape(2, PLANE, k8, n_i)
+
+    def x_of(v_mine, v_ref):
+        acc = None
+        for i in range(2):
+            v_i = (v_ref[i, 1] if v_mine else v_ref[i]).reshape(n_k, n_c)
+            d = lax.dot_general(v_i, tl[:, i].reshape(n_i, n_c), dn, preferred_element_type=F32)
+            acc = d if acc is None else acc + d
+        return acc.reshape(PLANE, k8, n_i)
+
+    x_part[core] = x_of(True, hv)
+    x_part[1 - core] = x_of(False, vo)
 
     def x_copy(k):
         qd = (q + k) % PLANE
-        return _rc(x_part.at[:, qd], x_in.at[q], x_s.at[k], x_r.at[k], (x, qd * 2 + core))
+        return _rc(x_part.at[:, qd], x_in.at[q], x_s, x_r, (x, qd * 2 + core))
 
     for k in range(1, PLANE):
         x_copy(k).start()
     x_in[q] = x_part[:, q]
-    a0.wait_recv()
-    a2 = a2()
-    a2.start()
-    a1.wait_recv()
-    a3 = a3()
-    a3.start()
-    b0.wait_recv()
-    b2 = b2()
-    b2.start()
-    b1.wait_recv()
-    b3 = b3()
-    b3.start()
-
-    for k in range(1, PLANE):
-        x_copy(k).wait_recv()
+    others = x_in.at[pl.ds(0, PLANE - 1)]
+    pltpu.make_async_copy(others, others, x_r).wait()
     xs = x_in[0]
     for k in range(1, PLANE):
         xs = xs + x_in[k]
@@ -234,6 +223,8 @@
 
     for k in range(1, RING):
         m_copy(k).start()
+    b0.start()
+    b1.start()
 
     def s_copy(i, k):
         xd = (x + k) % RING
@@ -259,13 +250,14 @@
         for k in range(lo, hi):
             ps_copy(k).start()
 
-    def s_work():
-        n1 = l1.shape[0]
-        quarter = n_v // RING
+    n1 = l1.shape[0]
+    quarter = n_v // RING
+
+    def r3_work(a_fwd):
         own1.wait()
         own2.wait()
-        a2.wait_recv()
-        a3.wait_recv()
+        for c in a_fwd:
+            c.wait_recv()
         acc = None
         kd = RING * n_v
         for i in range(2 * RING):
@@ -277,8 +269,10 @@
                 wd_copy(i + 2).start()
         for i in range(RING):
             d_n[quarter * i:quarter * (i + 1), :] = acc[n1 * i:n1 * i + quarter]
-        b2.wait_recv()
-        b3.wait_recv()
+
+    def r5_work(b_fwd):
+        for c in b_fwd:
+            c.wait_recv()
         acc = None
         kb = FULL * n_kd
         kh = kb // 2
@@ -329,27 +323,36 @@
         lo, hi = pl.ds(0, n), pl.ds(n, n)
         far, up, dn_ = (c + 2) % RING, (c + 1) % RING, (c + RING - 1) % RING
         ss, ww = (s1, w1) if first else (s2, w2)
+        last = isinstance(t, int) and t == N_CH
         srcs = (far, lo), (far, hi), (up, hi), (dn_, lo), (up, lo), (dn_, hi)
 
         def msg(i):
             d = 1 if i % 2 == 0 else RING - 1
-            return _rc(pb.at[pre + srcs[i]], rb.at[i], ss.at[t, i], ww.at[t, i], to(first, a, d))
+            return _rc(pb.at[pre + srcs[i]], rb.at[i], ss.at[int(last)], ww.at[t, min(i, 2)], to(first, a, d))
         return msg
 
-    near = range(2, 6)
+    def near(rb, ww, t):
+        got = rb.at[pl.ds(2, 4)]
+        pltpu.make_async_copy(got, got, ww.at[t, 2]).wait()
 
     def l1_step(t, a, pb, rb, c0, w):
         tp = t_pair[:, :, pl.ds(c0, w)].reshape(2 * rows, w)
         acc = jnp.dot(m_t[...], tp, preferred_element_type=F32)
         for i in range(2):
-            acc = acc + jnp.dot(tl[i].reshape(n_i, n_c), v_buf[i, :, pl.ds(c0, w)], preferred_element_type=F32)
+            acc = acc + jnp.dot(tl[:, i].reshape(n_i, n_c), v_buf[i, :, pl.ds(c0, w)], preferred_element_type=F32)
         for zb in range(RING):
             for yb in range(RING):
-                b = (zb * RING + yb) * rows
-                pb[yb * a + zb * (1 - a), zb * a + yb * (1 - a)] = acc[b:b + rows]
+                for i in range(RING):
+                    b = i * n_k + (zb * RING + yb) * k8
+                    pb[yb * a + zb * (1 - a), zb * a + yb * (1 - a), i * k8:(i + 1) * k8] = acc[b:b + k8]
         msg = stage(True, t, a, pb, rb)
-        for i in range(4):
-            msg(i).start()
+        msg(0).start()
+        msg(1).start()
+
+    def plain_step(t, a, pb, rb):
+        msg = stage(True, t, a, pb, rb)
+        msg(2).start()
+        msg(3).start()
 
     def add_step(first, t, a, pb, rb):
         u, v = coords(a)
@@ -366,9 +369,7 @@
 
     def l3_step(t, a, pb, rb, rb2):
         u, _ = coords(a)
-        msg = stage(True, t, a, pb, rb)
-        for i in near:
-            msg(i).wait_recv()
+        near(rb, w1, t)
         pb[u, :2] = pb[u, :2] + rb[4] + rb[3]
         pb[u, 2:] = pb[u, 2:] + rb[2] + rb[5]
         nxt = stage(False, t, a, pb, rb2)
@@ -381,16 +382,11 @@
     def l5_step(t, a, pb, rb, rb2, c0, w):
         u, v = coords(a)
         h = rows // 2
-        msg, old = stage(False, t, a, pb, rb2), stage(True, t, a, pb, rb)
-        for i in near:
-            msg(i).wait_recv()
+        near(rb2, w2, t)
         sym = s1_in[:, :, pl.ds(c0, w)].reshape(rows, w) + ps_in[:, pl.ds(c0, w)]
         out[:h, pl.ds(c0, w)] = pb[u, v, :h] + rb2[4] + rb2[3] + sym[:h]
         out[h:, pl.ds(c0, w)] = pb[u, v, h:] + rb2[2] + rb2[5] + sym[h:]
         o_copy(t, c0, w).start()
-        for i in range(6):
-            msg(i).wait_send()
-            old(i).wait_send()
 
     def at(t):
         return (t, 1 - t % 2, p_b.at[t], r1.at[t], r2.at[t])
@@ -403,10 +399,6 @@
 
     tail = (N_CH, 1, p_t, r1t, r2t)
     ct = N_CH * CW
-
-    def each(p, fn):
-        for i in range(2):
-            fn(2 * p + i)
 
     def run1(t):
         n, a, pb, rb, _ = at(t)
@@ -422,28 +414,24 @@
         n, a, pb, _, rb2 = at(t)
         add_step(False, n, a, pb, rb2)
 
-    pairs = N_CH // 2
-    loop(0, run1, 2 * EARLY)
+    loop(0, run1, EARLY)
+    b_fwd = onward(b0, b1, b2, b3)
+    loop(EARLY, run1)
     l1_step(*tail[:4], ct, TAIL)
-    s_work()
+    loop(0, lambda t: plain_step(*at(t)[:4]))
+    plain_step(*tail[:4])
+    r3_work(a_fwd)
+    loop(0, run2)
     add_step(True, *tail[:4])
-
-    def pair_step(p):
-        each(p, run2)
-        pl.when(p + EARLY < pairs)(lambda: each(p + EARLY, run1))
-        pl.when(p >= 1)(lambda: each(p - 1, run3))
-        pl.when(p >= 2)(lambda: each(p - 2, run4))
-
-    lax.fori_loop(0, pairs, lambda p, c: (pair_step(p), c)[1], 0)
+    r5_work(b_fwd)
+    loop(0, run3, EARLY + 1)
     ps_ready()
-    ps_send(1, 12)
+    ps_send(1, ROWS)
+    loop(EARLY + 1, run3)
     l3_step(*tail)
-    each(pairs - 2, run4)
-    each(pairs - 1, run3)
+    loop(0, run4, EARLY + 1)
+    loop(EARLY + 1, run4)
     add_step(False, *tail[:3], r2t)
-    ps_send(12, 22)
-    each(pairs - 1, run4)
-    ps_send(22, ROWS)
     s_own[0].wait()
     ps_own.wait()
     for k in range(1, RING):
@@ -455,19 +443,15 @@
     for i in range(N_CH + 1):
         o_copy(i, i * CW, CW if i < N_CH else TAIL).wait()
 
-    for c in (g0, g1, g2, g3, a0, a1, a2, a3, b0, b1, b2, b3):
+    for sem, bufs in ((s1, (r1, r1t)), (s2, (r2, r2t))):
+        for i in range(2):
+            pltpu.make_async_copy(bufs[i], bufs[i], sem.at[i]).wait()
+    for c in (g0, g1, g2, g3, a0, a1, b0, b1, *a_fwd, *b_fwd):
         c.wait_send()
-    for rel in range(RING):
-        xs = (x + rel) % RING
-        for k in range(RING):
-            c = t_copy(xs, (y + k) % RING)
-            if k == 0:
-                pl.when(xs != z)(c.wait_send)
-            else:
-                c.wait_send()
-    v_each(lambda c: c.wait_send(), None)
-    for k in range(1, PLANE):
-        x_copy(k).wait_send()
+    pltpu.make_async_copy(t_others, t_others, t_s).wait()
+    for k in range(1, RING):
+        h_copy(k).wait_send()
+    pltpu.make_async_copy(others, others, x_s).wait()
     for k in range(1, RING):
         m_copy(k).wait_send()
         s_copy(0, k).wait_send()
@@ -476,8 +460,9 @@
         ps_copy(k).wait_send()
 
 
-def sweep_call(ts, l1, l2, vs, wd, wx, v, t2, oo):
-    n_p, rows, n_c = ts.shape
+def sweep_call(tv, l1, l2, wd, wx, v, t2, oo):
+    n_p, n_c = tv.shape[1], tv.shape[4]
+    rows = t2.shape[0]
     n_k, n_v, n_j = wd.shape
     cols = t2.shape[1]
     k8 = rows // RING
@@ -497,18 +482,17 @@
     def sems(*shape):
         return dma(shape)
 
-    one, two, four, six = (), (2,), (RING,), (n, 6)
-    all16, sq = (PLANE,), (RING, RING)
+    one, two, four, six = (), (2,), (RING,), (n, 3)
     v9 = (-(-cols // 640),)
-    counts = [four, four, sq, all16, four, four, four, four, sq, all16, one, one, (8,), two, two, two,
-              v9, v9, v9, one, one, all16, all16, four, four, six, six, six, six, (2, RING), (2, RING), (ROWS,), (ROWS,), (n,), two]
+    counts = [four, four, four, four, one, one, four, four, four, four, one, one, (8,), two, two, two,
+              v9, v9, v9, one, one, one, one, four, four, two, six, two, six, (2, RING), (2, RING), (ROWS,), (ROWS,), (n,), two]
     return pl.pallas_call(
         sweep_kernel,
         out_shape=jax.ShapeDtypeStruct((rows, cols), F32),
-        in_specs=[vm, vm, vm, vm, hbm, hbm, hbm, vm, hbm],
+        in_specs=[vm, vm, vm, hbm, hbm, hbm, vm, hbm],
         out_specs=hbm,
         scratch_shapes=[
-            b16(RING, n_p, rows, n_c), b16(2, PLANE, rows, n_c), b16(2, 2, PLANE, k8, n_c),
+            b16(*tv.shape), b16(2, 2, PLANE, k8, n_c), b16(2, PLANE, k8, n_c), b16(RING, 2, PLANE, k8, n_c),
             b16(RING, *l1.shape), b16(RING, *l2.shape),
             b16(2, RING, n_v, n_j), b16(2, n_k // 2, FULL, n_j), b16(2, n_k, EDGE, n_j),
             f32(n_v, n_j), f32(n_v, n_j), f32(k8, n_v, n_v), f32(k8, n_v, n_v), f32(2, *blk), f32(*blk), f32(*blk), f32(rows, cols), f32(rows, cols), b16(2, k8, 2 * n_i), f32(2, k8, n_i),
@@ -520,7 +504,7 @@
         ] + [sems(*c) if c else dma for c in counts],
         compiler_params=pltpu.CompilerParams(has_side_effects=True, collective_id=0, vmem_limit_bytes=VMEM_LIMIT),
         name="sweep",
-    )(ts, l1, l2, vs, wd, wx, v, t2, oo)
+    )(tv, l1, l2, wd, wx, v, t2, oo)
 
 
 def solution(mesh):
@@ -538,8 +522,7 @@
         n_p = cols_dev // c_dev
         x = lax.axis_index("col")
         t_half = t_blk.astype(BF16)
-        ts = t_half.reshape(rows_dev, n_p, c_dev).transpose(1, 0, 2)
-        vs = oovv_blk.reshape(n_col, occ_col, n_p, c_dev).transpose(2, 0, 1, 3)
+        tv = jnp.stack([a.reshape(n_col, occ_col, n_p, c_dev).transpose(0, 2, 1, 3) for a in (t_half, oovv_blk)], axis=2)
         t3 = t_half.reshape(n_occ, virt_col, n_virt)
         l1 = t3.transpose(1, 0, 2).reshape(virt_col, n_occ * n_virt)
         l1 = jnp.pad(l1, ((0, 12), (0, 0)))
@@ -552,7 +535,7 @@
         l2 = jnp.concatenate([full, edge.reshape(n_virt, n_occ * EDGE)], axis=1)
         wd3 = wd_blk.reshape(n_occ, n_virt, occ_col * n_virt)
         wx3 = wx_blk.reshape(n_occ, n_virt, occ_col * n_virt)
-        summed = sweep_call(ts, l1, l2, vs, wd3, wx3, vvvv_blk, t_half, oooo_full)
+        summed = sweep_call(tv, l1, l2, wd3, wx3, vvvv_blk, t_half, oooo_full)
         return (oovv_blk.astype(F32) + summed) / d_blk
 
     return jax.shard_map(local_sweep, mesh=mesh, in_specs=(amp_spec, amp_spec, amp_spec, amp_spec, P(), wide_spec, wide_spec), out_specs=amp_spec, check_vma=False)

time: 152 us -> 139 us (0.914)
  Pallas kernels: 140 us -> 128 us
    pallas_call x1, Pallas kernels: 140 us -> 128 us  [sweep_call(): pl.pallas_call(sweep_kernel, out_shape=jax.ShapeDtypeStruct((rows, cols),...]
where the time goes in v6:
time: 139 us; the launch traced here: 138 us
  Pallas kernels  128 us (92%)
  other arithmetic  5.4 us (4%)
  local copies, waits for them, and re-layouts  5.33 us (4%)
    pallas_call x1, Pallas kernels, sweep_call(): pl.pallas_call(sweep_kernel, out_shape=jax.ShapeDtypeStruct((rows, cols),...  128 us

profile of v6, /device:TPU:0, one launch (start us, length us, event | category | flops | bytes accessed | tf_op | source)
XLA Modules:
  0.0 138.4 jit_solution(14873566377026556680)
XLA Ops:
  0.0 1.1 convert_element_type.9.t2
  1.1 0.0 copy-start
  1.1 0.7 reshape.24
  1.8 1.7 %reshape.25 = bf16[4,8,8,648]{3,2,1,0:T(8,128)(2,1)S(1)} reshape(bf16[32,5184]{1,0:T(8,128)(2,1)} %param.9) | data formatting | bytes 663552 | tf_op jit(solution)/shard_map/reshape | solution.py:525
  3.5 0.1 copy_bitcast_fusion
  3.7 1.0 pad_maximum_fusion.tv
  4.6 0.8 reshape.26
  5.5 0.1 select_bitcast_fusion
  5.5 0.1 copy.16
  5.7 0.1 slice_select_fusion
  5.8 0.2 copy.15
  6.0 0.8 pad_maximum_fusion.1.l2
  6.7 0.1 copy.14
  6.9 0.0 copy-done
  6.9 0.8 reshape.27
  7.7 0.8 pad.6.l1
  8.5 127.6 %sweep.1 = f32[32,5184]{1,0:T(8,128)} custom-call(bf16[4,8,2,8,648]{4,3,2,1,0:T(8,128)(2,1)} %pad_maximum_fusion.tv, bf16[48,4608]{1,0:T(8,128)(2,1)} %pad.6.l1, bf16[144,1280]{1,0:T(8,128)(2,1)} %pad_maximum_fusion.1.l2, bf16[32,144,1152]{2,1,0:T(8,128)(2,1)} %bitcast.15, bf16[32,144,1152]{2,1,0:T(8,128)(2,1)} %bitcast.16, bf16[648,5184]{1,0:T(8,128)(2,1)} %v_hbm.1, ...), custom_call_target="tpu_custom_call" | custom-call | tf_op jit(solution)/shard_map/sweep/pallas_call | solution.py:489
  136.1 2.3 %add_divide_fusion = f32[32,5184]{1,0:T(8,128)} fusion(f32[32,5184]{1,0:T(8,128)} %param.8, f32[32,5184]{1,0:T(8,128)} %sweep.1, bf16[32,5184]{1,0:T(8,128)(2,1)} %param.9), kind=kLoop, calls=%fused_computation.1 | loop fusion | flops 497664 | bytes 2322432 | tf_op jit(solution)/shard_map/div | solution.py:539
  (1 shorter events, 0.0 us)
Async XLA Ops:
  1.1 5.7 %copy-start = (bf16[32,5184]{1,0:T(8,128)(2,1)}, bf16[32,5184]{1,0:T(8,128)(2,1)S(1)}, u32[]{:S(2)}) copy-start(bf16[32,5184]{1,0:T(8,128)(2,1)S(1)} %convert_element_type.9.t2) | copy-start | bytes 995332

commit v7 on v6

--- a/solution.py
+++ b/solution.py
@@ -47,7 +47,8 @@
     pl.semaphore_wait(bar, RING - 1 + ROWS - 1)
 
 
-def sweep_kernel(tv, l1, l2, wd, wx, v_hbm, t2, oo_hbm, out_hbm,
+def sweep_kernel(t_in, ov_in, wd, wx, v_hbm, oo_hbm, out_hbm,
+                 tv, l1, l2, t2,
                  h_in, hv, vo, tl, lg1, lg2, wdb, wxb, wxs, d_n, e_n, s_f, s_b, sw, s1_in, s2_in, ps_in, out, oo2, oo, v_buf, t_pair, m_t, x_part, x_in, m_all,
                  p_b, p_t, r1, r1t, r2, r2t,
                  g_s, g_r, h_s, h_r, t_s, t_r, p_s, p_r, o_s, o_r, f_s, f_r, loc, wd_s, wx_s, wy_s,
@@ -59,6 +60,13 @@
     k8, n_c = tl.shape[3:]
     rows = RING * k8
     loc_g, loc_t, loc_1, loc_2, loc_v, loc_p, loc_a, loc_b = [loc.at[i] for i in range(loc.shape[0])]
+
+    t2[...] = t_in[...].astype(BF16)
+    for xd in range(RING):
+        rq = slice(xd * k8, (xd + 1) * k8)
+        for i, val in enumerate((t_in[rq, :], ov_in[rq, :].astype(F32))):
+            for p in range(tv.shape[1]):
+                tv[xd, p, i] = val[:, p * n_c:(p + 1) * n_c].astype(BF16)
     _enter(x, r)
 
     def ring(src, buf, ss, rr, axis):
@@ -83,8 +91,6 @@
 
     for k in (1, RING - 1, 2):
         h_copy(k).start()
-    own1.start()
-    own2.start()
 
     def onward(r0, r1_, f0, f1):
         r0.wait_recv()
@@ -137,6 +143,29 @@
                 t_copy(xs, yd, buf).start()
 
     t_block(0)
+    quarter = n_v // RING
+    groups = t2.shape[0] // EDGE
+    for a in range(quarter):
+        for kk in range(groups):
+            s_f[:, quarter * kk + a, :] = t_in[EDGE * kk:EDGE * (kk + 1), n_v * a:n_v * (a + 1)]
+    rest = quarter - FULL
+    odd = x % 2 == 1
+    none = jnp.zeros((n_v, EDGE - rest), F32)
+    for k in range(t2.shape[0]):
+        kk = k // EDGE
+        bt = s_f[k % EDGE, quarter * kk:quarter * (kk + 1), :].T
+        e_n[:, FULL * k:FULL * (k + 1)] = jnp.where(odd, bt[:, rest:], bt[:, :FULL])
+        d_n[:, EDGE * k:EDGE * (k + 1)] = jnp.where(odd, jnp.concatenate([none, bt[:, :rest]], axis=1), jnp.concatenate([bt[:, FULL:], none], axis=1))
+    l2[:, :FULL * n_kd] = e_n[:, :FULL * n_kd].astype(BF16)
+    l2[:, FULL * n_kd:] = d_n[:, :EDGE * n_kd].astype(BF16)
+    pad1 = l1.shape[0]
+    d_n[:pad1, :] = jnp.zeros((pad1, n_j), F32)
+    for kk in range(groups):
+        for i in range(EDGE):
+            d_n[:quarter, n_v * i:n_v * (i + 1)] = s_f[i, quarter * kk:quarter * (kk + 1), :]
+        l1[:, n_j * kk:n_j * (kk + 1)] = d_n[:pad1, :].astype(BF16)
+    own1.start()
+    own2.start()
     a0, a1, a2, a3 = ring(l1, lg1, p_s, p_r, 1)
     b0, b1, b2, b3 = ring(l2, lg2, o_s, o_r, 1)
     a0.start()
@@ -251,7 +280,6 @@
             ps_copy(k).start()
 
     n1 = l1.shape[0]
-    quarter = n_v // RING
 
     def r3_work(a_fwd):
         own1.wait()
@@ -460,15 +488,18 @@
         ps_copy(k).wait_send()
 
 
-def sweep_call(tv, l1, l2, wd, wx, v, t2, oo):
-    n_p, n_c = tv.shape[1], tv.shape[4]
-    rows = t2.shape[0]
+def sweep_call(t_blk, oovv, wd, wx, v, oo):
+    rows, cols = t_blk.shape
+    n_c = v.shape[0]
+    n_p = cols // n_c
     n_k, n_v, n_j = wd.shape
-    cols = t2.shape[1]
     k8 = rows // RING
     n_i = PLANE * rows
     blk = (RING, k8, cols)
     n = N_CH + 1
+    pad1 = 48
+    tv_shape = (RING, n_p, 2, k8, n_c)
+    l1_shape, l2_shape = (pad1, n_k * n_v), (n_v, n_k * (FULL + EDGE))
     dma = pltpu.SemaphoreType.DMA
     vm = pl.BlockSpec(memory_space=pltpu.VMEM)
     hbm = pl.BlockSpec(memory_space=pl.ANY)
@@ -489,11 +520,12 @@
     return pl.pallas_call(
         sweep_kernel,
         out_shape=jax.ShapeDtypeStruct((rows, cols), F32),
-        in_specs=[vm, vm, vm, hbm, hbm, hbm, vm, hbm],
+        in_specs=[vm, vm, hbm, hbm, hbm, hbm],
         out_specs=hbm,
         scratch_shapes=[
-            b16(*tv.shape), b16(2, 2, PLANE, k8, n_c), b16(2, PLANE, k8, n_c), b16(RING, 2, PLANE, k8, n_c),
-            b16(RING, *l1.shape), b16(RING, *l2.shape),
+            b16(*tv_shape), b16(*l1_shape), b16(*l2_shape), b16(rows, cols),
+            b16(*tv_shape), b16(2, 2, PLANE, k8, n_c), b16(2, PLANE, k8, n_c), b16(RING, 2, PLANE, k8, n_c),
+            b16(RING, *l1_shape), b16(RING, *l2_shape),
             b16(2, RING, n_v, n_j), b16(2, n_k // 2, FULL, n_j), b16(2, n_k, EDGE, n_j),
             f32(n_v, n_j), f32(n_v, n_j), f32(k8, n_v, n_v), f32(k8, n_v, n_v), f32(2, *blk), f32(*blk), f32(*blk), f32(rows, cols), f32(rows, cols), b16(2, k8, 2 * n_i), f32(2, k8, n_i),
             b16(2, n_c, cols), b16(2, rows, cols), b16(n_i, 2 * rows),
@@ -504,7 +536,7 @@
         ] + [sems(*c) if c else dma for c in counts],
         compiler_params=pltpu.CompilerParams(has_side_effects=True, collective_id=0, vmem_limit_bytes=VMEM_LIMIT),
         name="sweep",
-    )(tv, l1, l2, wd, wx, v, t2, oo)
+    )(t_blk, oovv, wd, wx, v, oo)
 
 
 def solution(mesh):
@@ -517,25 +549,9 @@
         n_occ = math.isqrt(oooo_full.shape[0])
         n_virt = wd_blk.shape[0] // n_occ
         occ_col = n_occ // n_col
-        virt_col = n_virt // n_col
-        c_dev = vvvv_blk.shape[0]
-        n_p = cols_dev // c_dev
-        x = lax.axis_index("col")
-        t_half = t_blk.astype(BF16)
-        tv = jnp.stack([a.reshape(n_col, occ_col, n_p, c_dev).transpose(0, 2, 1, 3) for a in (t_half, oovv_blk)], axis=2)
-        t3 = t_half.reshape(n_occ, virt_col, n_virt)
-        l1 = t3.transpose(1, 0, 2).reshape(virt_col, n_occ * n_virt)
-        l1 = jnp.pad(l1, ((0, 12), (0, 0)))
-        tb = t3.transpose(2, 0, 1)
-        odd = x % 2 == 1
-        rest = virt_col - FULL
-        gap = jnp.zeros((n_virt, n_occ, EDGE - rest), BF16)
-        full = jnp.where(odd, tb[:, :, rest:], tb[:, :, :FULL]).reshape(n_virt, n_occ * FULL)
-        edge = jnp.where(odd, jnp.concatenate([gap, tb[:, :, :rest]], axis=2), jnp.concatenate([tb[:, :, FULL:], gap], axis=2))
-        l2 = jnp.concatenate([full, edge.reshape(n_virt, n_occ * EDGE)], axis=1)
         wd3 = wd_blk.reshape(n_occ, n_virt, occ_col * n_virt)
         wx3 = wx_blk.reshape(n_occ, n_virt, occ_col * n_virt)
-        summed = sweep_call(tv, l1, l2, wd3, wx3, vvvv_blk, t_half, oooo_full)
+        summed = sweep_call(t_blk, oovv_blk, wd3, wx3, vvvv_blk, oooo_full)
         return (oovv_blk.astype(F32) + summed) / d_blk
 
     return jax.shard_map(local_sweep, mesh=mesh, in_specs=(amp_spec, amp_spec, amp_spec, amp_spec, P(), wide_spec, wide_spec), out_specs=amp_spec, check_vma=False)

time: 139 us -> 132 us (0.950)
  local copies, waits for them, and re-layouts: 5.33 us -> 0 us
  other arithmetic: 5.4 us -> 2.32 us
    reshape x6 -> x0, local copies, waits for them, and re-layouts: 4.22 us -> none  [the longest x2 2.35 us: local_sweep(): a.reshape(n_col, occ_col, n_p, c_dev).transpose(0, 2, 1, 3)]
    pallas_call x1, Pallas kernels: 128 us -> 129 us  [sweep_call(): pl.pallas_call(sweep_kernel, out_shape=jax.ShapeDtypeStruct((rows, cols),...]
where the time goes in v7:
time: 132 us
  Pallas kernels  129 us (98%)
  other arithmetic  2.32 us (2%)
    pallas_call x1, Pallas kernels, sweep_call(): pl.pallas_call(sweep_kernel, out_shape=jax.ShapeDtypeStruct((rows, cols),...  129 us

profile of v7, /device:TPU:0, one launch (start us, length us, event | category | flops | bytes accessed | tf_op | source)
XLA Modules:
  0.0 131.7 jit_solution(8916468965271913804)
XLA Ops:
  0.0 129.4 %sweep.1 = f32[32,5184]{1,0:T(8,128)} custom-call(f32[32,5184]{1,0:T(8,128)} %t_in.1, bf16[32,5184]{1,0:T(8,128)(2,1)} %ov_in.1, bf16[32,144,1152]{2,1,0:T(8,128)(2,1)} %bitcast.2, bf16[32,144,1152]{2,1,0:T(8,128)(2,1)} %bitcast.3, bf16[648,5184]{1,0:T(8,128)(2,1)} %v_hbm.1, bf16[1024,1024]{1,0:T(8,128)(2,1)} %oo_hbm.1), custom_call_target="tpu_custom_call" | custom-call | tf_op jit(solution)/shard_map/sweep/pallas_call | solution.py:520
  129.4 2.3 %add_divide_fusion = f32[32,5184]{1,0:T(8,128)} fusion(f32[32,5184]{1,0:T(8,128)} %param.8, f32[32,5184]{1,0:T(8,128)} %sweep.1, bf16[32,5184]{1,0:T(8,128)(2,1)} %ov_in.1), kind=kLoop, calls=%fused_computation | loop fusion | flops 497664 | bytes 2322432 | tf_op jit(solution)/shard_map/div | solution.py:555

commit v8 on v7

--- a/solution.py
+++ b/solution.py
@@ -47,7 +47,7 @@
     pl.semaphore_wait(bar, RING - 1 + ROWS - 1)
 
 
-def sweep_kernel(t_in, ov_in, wd, wx, v_hbm, oo_hbm, out_hbm,
+def sweep_kernel(t_in, ov_in, d_in, wd, wx, v_hbm, oo_hbm, out_hbm,
                  tv, l1, l2, t2,
                  h_in, hv, vo, tl, lg1, lg2, wdb, wxb, wxs, d_n, e_n, s_f, s_b, sw, s1_in, s2_in, ps_in, out, oo2, oo, v_buf, t_pair, m_t, x_part, x_in, m_all,
                  p_b, p_t, r1, r1t, r2, r2t,
@@ -412,8 +412,9 @@
         h = rows // 2
         near(rb2, w2, t)
         sym = s1_in[:, :, pl.ds(c0, w)].reshape(rows, w) + ps_in[:, pl.ds(c0, w)]
-        out[:h, pl.ds(c0, w)] = pb[u, v, :h] + rb2[4] + rb2[3] + sym[:h]
-        out[h:, pl.ds(c0, w)] = pb[u, v, h:] + rb2[2] + rb2[5] + sym[h:]
+        sym = sym + ov_in[:, pl.ds(c0, w)].astype(F32)
+        out[:h, pl.ds(c0, w)] = (pb[u, v, :h] + rb2[4] + rb2[3] + sym[:h]) / d_in[:h, pl.ds(c0, w)]
+        out[h:, pl.ds(c0, w)] = (pb[u, v, h:] + rb2[2] + rb2[5] + sym[h:]) / d_in[h:, pl.ds(c0, w)]
         o_copy(t, c0, w).start()
 
     def at(t):
@@ -488,7 +489,7 @@
         ps_copy(k).wait_send()
 
 
-def sweep_call(t_blk, oovv, wd, wx, v, oo):
+def sweep_call(t_blk, oovv, den, wd, wx, v, oo):
     rows, cols = t_blk.shape
     n_c = v.shape[0]
     n_p = cols // n_c
@@ -520,7 +521,7 @@
     return pl.pallas_call(
         sweep_kernel,
         out_shape=jax.ShapeDtypeStruct((rows, cols), F32),
-        in_specs=[vm, vm, hbm, hbm, hbm, hbm],
+        in_specs=[vm, vm, vm, hbm, hbm, hbm, hbm],
         out_specs=hbm,
         scratch_shapes=[
             b16(*tv_shape), b16(*l1_shape), b16(*l2_shape), b16(rows, cols),
@@ -536,7 +537,7 @@
         ] + [sems(*c) if c else dma for c in counts],
         compiler_params=pltpu.CompilerParams(has_side_effects=True, collective_id=0, vmem_limit_bytes=VMEM_LIMIT),
         name="sweep",
-    )(t_blk, oovv, wd, wx, v, oo)
+    )(t_blk, oovv, den, wd, wx, v, oo)
 
 
 def solution(mesh):
@@ -551,7 +552,6 @@
         occ_col = n_occ // n_col
         wd3 = wd_blk.reshape(n_occ, n_virt, occ_col * n_virt)
         wx3 = wx_blk.reshape(n_occ, n_virt, occ_col * n_virt)
-        summed = sweep_call(t_blk, oovv_blk, wd3, wx3, vvvv_blk, oooo_full)
-        return (oovv_blk.astype(F32) + summed) / d_blk
+        return sweep_call(t_blk, oovv_blk, d_blk, wd3, wx3, vvvv_blk, oooo_full)
 
     return jax.shard_map(local_sweep, mesh=mesh, in_specs=(amp_spec, amp_spec, amp_spec, amp_spec, P(), wide_spec, wide_spec), out_specs=amp_spec, check_vma=False)

time: 132 us -> 132 us (level)
  other arithmetic: 2.32 us -> 0 us
  local copies, waits for them, and re-layouts: 0 us -> 1.98 us
    div x1 -> x0, other arithmetic: 2.32 us -> none  [local_sweep(): return (oovv_blk.astype(F32) + summed) / d_blk]
    unnamed x0 -> x1, local copies, waits for them, and re-layouts: none -> 1.98 us
where the time goes in v8:
time: 132 us
  Pallas kernels  130 us (98%)
  local copies, waits for them, and re-layouts  1.98 us (2%)
    pallas_call x1, Pallas kernels, sweep_call(): pl.pallas_call(sweep_kernel, out_shape=jax.ShapeDtypeStruct((rows, cols),...  130 us

profile of v8, /device:TPU:0, one launch (start us, length us, event | category | flops | bytes accessed | tf_op | source)
XLA Modules:
  0.0 131.7 jit_solution(213371512117006506)
XLA Ops:
  0.0 129.7 %sweep.1 = f32[32,5184]{1,0:T(8,128)} custom-call(f32[32,5184]{1,0:T(8,128)} %t_in.1, bf16[32,5184]{1,0:T(8,128)(2,1)} %ov_in.1, f32[32,5184]{1,0:T(8,128)} %d_in.1, bf16[32,144,1152]{2,1,0:T(8,128)(2,1)} %bitcast.2, bf16[32,144,1152]{2,1,0:T(8,128)(2,1)} %bitcast.3, bf16[648,5184]{1,0:T(8,128)(2,1)} %v_hbm.1, bf16[1024,1024]{1,0:T(8,128)(2,1)} %oo_hbm.1), custom_call_target="tpu_custom_call" | custom-call | tf_op jit(solution)/shard_map/sweep/pallas_call | solution.py:521
  129.7 2.0 %copy.9 = f32[32,5184]{1,0:T(8,128)} copy(f32[32,5184]{1,0:T(8,128)} %sweep.1) | data formatting | bytes 1327104
